TPU v7x, 128 devices: a whole 4x4x4 slice. The times are simulated.
128 devices in a mesh: row: 16 (over x, z_hi, core), col: 8 (over y, z_lo).
Axes of the slice: x: 4, y: 4, z: 4 (z_hi: 2, z_lo: 2; z = z_hi * 2 + z_lo), core: 2. Of those that a mesh axis runs over, the one named last changes fastest.
Arguments:
- velocity: float32 [3, 2, 128, 256, 256], P(None, None, 'row', 'col'), may hold values from -7.5 to 7.5
- accumulator: float32 [3, 2, 128, 256, 256], P(None, None, 'row', 'col'), may hold values from -6 to 6
- remesh_flag: int32 [128], P('row'), may hold values 0 or 1
- remesh_shift: int32 [128], P('row'), may hold values from -128 to 127
- viscosity: float32 [1], replicated, may hold values from 0.0003 to 0.0015
- shear: float32 [1], replicated, may hold values from 8 to 20
- clock: float32 [1], replicated, may hold values from 0 to 0.05
- step: float32 [1], replicated, may hold values from 0.004 to 0.01
Outputs:
- new_velocity: float32 [3, 2, 128, 256, 256], P(None, None, 'row', 'col')
- new_accumulator: float32 [3, 2, 128, 256, 256], P(None, None, 'row', 'col')
- spectra: float32 [2, 128], P(None, 'row')
All inputs are finite; a program needn't handle non-finite values. No bound on the sum of `remesh_flag` on one device may be relied on, other than what follows from the above.
Results may differ from a plain program's by a relative error of at most 0.0001.
Values sent between devices are 32-bit elements; how exact they have to be, the bound alone decides.
A program may use at most 192 MiB of HBM per device.

v0:
```python
import math

import jax
import jax.numpy as jnp
from jax import lax
from jax.sharding import PartitionSpec as P

NX = 256
NY = 256
NZ = 256


def signed_index(positions, period):
    return jnp.where(2 * positions < period, positions, positions - period)


def roll_rows(field, amounts):

    def shift_row(row_data, amount_one):
        return jnp.roll(row_data, -amount_one, axis=-1)

    return jax.vmap(shift_row, in_axes=(2, 0), out_axes=2)(field, amounts)


def dft_tables(period):
    positions = jnp.arange(period, dtype=jnp.int32)
    product = positions[:, None] * positions[None, :] % period
    angles = product.astype(jnp.float32) * (2.0 * math.pi / period)
    factor = 1.0 / math.sqrt(period)
    return (jnp.cos(angles) * factor, jnp.sin(angles) * factor)


def product_high(formula, first_arg, second_arg):
    return jnp.einsum(formula, first_arg, second_arg, precision=lax.Precision.HIGHEST)


def rotate(left_side, right_side, output, real_part, imag_part, cosine_table, sine_table, backward):
    stacked = jnp.stack([real_part, imag_part])
    if backward:
        block_table = jnp.stack(
            [jnp.stack([cosine_table, sine_table]), jnp.stack([-sine_table, cosine_table])]
        )
    else:
        block_table = jnp.stack(
            [jnp.stack([cosine_table, -sine_table]), jnp.stack([sine_table, cosine_table])]
        )
    result = product_high(
        "s" + left_side + ",st" + right_side + "->t" + output, stacked, block_table
    )
    return (result[0], result[1])


def project(real_part, imag_part, wave_vector, inverse_square):
    along_real = (
        wave_vector[0] * real_part[0]
        + wave_vector[1] * real_part[1]
        + wave_vector[2] * real_part[2]
    ) * inverse_square
    along_imag = (
        wave_vector[0] * imag_part[0]
        + wave_vector[1] * imag_part[1]
        + wave_vector[2] * imag_part[2]
    ) * inverse_square
    return (
        jnp.stack([real_part[number] - wave_vector[number] * along_real for number in range(3)]),
        jnp.stack([imag_part[number] - wave_vector[number] * along_imag for number in range(3)]),
    )


def cross_product(first_one, second_one):
    return jnp.stack(
        [
            first_one[1] * second_one[2] - first_one[2] * second_one[1],
            first_one[2] * second_one[0] - first_one[0] * second_one[2],
            first_one[0] * second_one[1] - first_one[1] * second_one[0],
        ]
    )


def to_physical(real_part, imag_part, tables_all):
    (cos_y, sin_y), (cos_x, sin_x), (cos_z, sin_z) = tables_all
    row_count = lax.axis_size("row")
    col_count = lax.axis_size("col")
    fields, width_x, width_z, full_y = real_part.shape
    block_y = full_y // row_count
    half_x = width_x * row_count
    full_x = cos_x.shape[0]
    block_x = full_x // col_count
    full_z = width_z * col_count
    shape_y = (full_y, row_count, block_y)
    first_real, first_imag = rotate(
        "fabc",
        "cpq",
        "fpabq",
        real_part,
        imag_part,
        cos_y.reshape(shape_y),
        sin_y.reshape(shape_y),
        True,
    )
    flat_shape = (fields, row_count, width_x, width_z * block_y)
    second_real, second_imag = (
        lax.all_to_all(
            first_real.reshape(flat_shape), "row", split_axis=1, concat_axis=2, tiled=True
        ),
        lax.all_to_all(
            first_imag.reshape(flat_shape), "row", split_axis=1, concat_axis=2, tiled=True
        ),
    )
    deep_shape = (fields, half_x, width_z, block_y)
    weights = jnp.where(jnp.arange(half_x) == 0, 1.0, 2.0).astype(jnp.float32)[:, None]
    shape_x = (half_x, col_count, block_x)
    cos_half = (weights * cos_x[:half_x]).reshape(shape_x)
    sin_half = (weights * sin_x[:half_x]).reshape(shape_x)
    third_real, third_imag = rotate(
        "fkzy",
        "kpq",
        "fpzyq",
        second_real.reshape(deep_shape),
        second_imag.reshape(deep_shape),
        cos_half,
        sin_half,
        True,
    )
    flat_shape = (fields, col_count, 1, width_z * block_y * block_x)
    fourth_real, fourth_imag = (
        lax.all_to_all(
            third_real.reshape(flat_shape), "col", split_axis=1, concat_axis=2, tiled=True
        ),
        lax.all_to_all(
            third_imag.reshape(flat_shape), "col", split_axis=1, concat_axis=2, tiled=True
        ),
    )
    deep_shape = (fields, col_count, width_z, block_y, block_x)
    shape_z = (col_count, width_z, full_z)
    stacked = jnp.stack([fourth_real.reshape(deep_shape), fourth_imag.reshape(deep_shape)])
    z_table = jnp.stack([cos_z.reshape(shape_z), -sin_z.reshape(shape_z)])
    return product_high("sfpkyq,spkn->fyqn", stacked, z_table)


def to_spectral(physical, tables_all, half_x):
    (cos_y, sin_y), (cos_x, sin_x), (cos_z, sin_z) = tables_all
    row_count = lax.axis_size("row")
    col_count = lax.axis_size("col")
    fields, block_y, block_x, full_z = physical.shape
    width_z = full_z // col_count
    width_x = half_x // row_count
    full_y = block_y * row_count
    shape_z = (full_z, col_count, width_z)
    z_table = jnp.stack([cos_z.reshape(shape_z), -sin_z.reshape(shape_z)])
    first_both = product_high("fyqn,tnpk->tfpkyq", physical, z_table)
    first_real, first_imag = (first_both[0], first_both[1])
    flat_shape = (fields, col_count, 1, width_z * block_y * block_x)
    second_real, second_imag = (
        lax.all_to_all(
            first_real.reshape(flat_shape), "col", split_axis=1, concat_axis=2, tiled=True
        ),
        lax.all_to_all(
            first_imag.reshape(flat_shape), "col", split_axis=1, concat_axis=2, tiled=True
        ),
    )
    deep_shape = (fields, col_count, width_z, block_y, block_x)
    shape_x = (col_count, block_x, row_count, width_x)
    third_real, third_imag = rotate(
        "fpkyq",
        "pqmr",
        "fmrky",
        second_real.reshape(deep_shape),
        second_imag.reshape(deep_shape),
        cos_x[:, :half_x].reshape(shape_x),
        sin_x[:, :half_x].reshape(shape_x),
        False,
    )
    flat_shape = (fields, row_count, 1, width_x * width_z * block_y)
    fourth_real, fourth_imag = (
        lax.all_to_all(
            third_real.reshape(flat_shape), "row", split_axis=1, concat_axis=2, tiled=True
        ),
        lax.all_to_all(
            third_imag.reshape(flat_shape), "row", split_axis=1, concat_axis=2, tiled=True
        ),
    )
    deep_shape = (fields, row_count, width_x, width_z, block_y)
    shape_y = (row_count, block_y, full_y)
    return rotate(
        "fparq",
        "pqn",
        "farn",
        fourth_real.reshape(deep_shape),
        fourth_imag.reshape(deep_shape),
        cos_y.reshape(shape_y),
        sin_y.reshape(shape_y),
        False,
    )


def many_physical(real_part, imag_part, tables_all):
    return to_physical(real_part, imag_part, tables_all)


def many_spectral(physical, tables_all, half_x):
    return to_spectral(physical, tables_all, half_x)


def body(velocity, accumulator, remesh_flag, remesh_shift, viscosity, shear, clock, step):
    width_x = velocity.shape[2]
    width_z = velocity.shape[3]
    full_y = velocity.shape[4]
    half_x = width_x * lax.axis_size("row")
    offset = remesh_flag * remesh_shift
    remeshed = roll_rows(velocity, offset)
    carried = roll_rows(accumulator, offset)
    lattice_x = lax.axis_index("row") * width_x + jnp.arange(width_x, dtype=jnp.int32)
    col_index = lax.axis_index("col") * width_z + jnp.arange(width_z, dtype=jnp.int32)
    lattice_z = signed_index(col_index, NZ)
    lattice_y = signed_index(jnp.arange(full_y, dtype=jnp.int32), NY)
    wave_x = lattice_x.astype(jnp.float32)[:, None, None]
    wave_z = lattice_z.astype(jnp.float32)[None, :, None]
    wave_y = lattice_y.astype(jnp.float32)[None, None, :] - shear[0] * clock[0] * wave_x
    wave_vector = (wave_x, wave_y, wave_z)
    square_wave = wave_x * wave_x + wave_y * wave_y + wave_z * wave_z
    inverse_square = 1.0 / jnp.maximum(square_wave, 1.0)
    dealias_mask = (
        (3 * lattice_x < NX)[:, None, None]
        & (3 * jnp.abs(lattice_z) < NZ)[None, :, None]
        & (3 * jnp.abs(lattice_y) < NY)[None, None, :]
    ).astype(jnp.float32)
    shear_rate = shear[0]
    viscous_rate = viscosity[0]
    stress_part = jnp.sum(
        remeshed[0, 0] * remeshed[1, 0] + remeshed[0, 1] * remeshed[1, 1], axis=(1, 2)
    )
    energy = jnp.sum(remeshed * remeshed, axis=(0, 1))
    dissipation_part = jnp.sum(square_wave * energy, axis=(1, 2))
    stress_total, dissipation_total = lax.psum((stress_part, dissipation_part), "col")
    solen_real, solen_imag = project(remeshed[:, 0], remeshed[:, 1], wave_vector, inverse_square)
    smooth_real = dealias_mask * solen_real
    smooth_imag = dealias_mask * solen_imag
    tables_all = (dft_tables(NY), dft_tables(NX), dft_tables(NZ))
    vort_real = -cross_product(wave_vector, smooth_imag)
    vort_imag = cross_product(wave_vector, smooth_real)
    both_real = jnp.concatenate([smooth_real, vort_real])
    both_imag = jnp.concatenate([smooth_imag, vort_imag])
    physical = many_physical(both_real, both_imag, tables_all)
    lamb_grid = cross_product(physical[:3], physical[3:])
    modes_real, modes_imag = many_spectral(lamb_grid, tables_all, half_x)
    hat_real = dealias_mask * modes_real
    hat_imag = dealias_mask * modes_imag
    proj_real, proj_imag = project(hat_real, hat_imag, wave_vector, inverse_square)
    coupling = 2.0 * shear_rate * wave_x * inverse_square

    def tendency(projected, state):
        term_list = [
            projected[number]
            + coupling * wave_vector[number] * state[1]
            - viscous_rate * square_wave * state[number]
            for number in range(3)
        ]
        term_list[0] = term_list[0] - shear_rate * state[1]
        return jnp.stack(term_list)

    tendencies = jnp.stack(
        [tendency(proj_real, remeshed[:, 0]), tendency(proj_imag, remeshed[:, 1])], axis=1
    )
    new_accumulator = -5.0 / 9.0 * carried + step[0] * tendencies
    new_velocity = remeshed + 15.0 / 16.0 * new_accumulator
    stress = stress_total / (NY * NZ)
    dissipation = 2.0 * viscous_rate * dissipation_total / (NY * NZ)
    return (new_velocity, new_accumulator, jnp.stack([stress, dissipation]))


def solution(mesh):
    in_specs = (
        P(None, None, "row", "col", None),
        P(None, None, "row", "col", None),
        P("row"),
        P("row"),
        P(),
        P(),
        P(),
        P(),
    )
    out_specs = (
        P(None, None, "row", "col", None),
        P(None, None, "row", "col", None),
        P(None, "row"),
    )
    return jax.shard_map(body, mesh=mesh, in_specs=in_specs, out_specs=out_specs, check_vma=False)
```

profile of v0, /device:TPU:1, one launch (start us, length us, event | category | flops | bytes accessed | tf_op | source)
XLA Modules:
  0.0 709.0 jit_solution(13609851444678728272)
XLA Ops:
  2.7 12.1 %copy.169 = f32[8,3,2,32,512]{3,1,2,0,4:T(4,128)} copy(f32[8,3,2,32,512]{4,3,2,1,0:T(8,128)S(1)} %pad_maximum_fusion) | data formatting | bytes 6291456 | tf_op jit(solution)/shard_map/vmap(jit(_roll_dynamic))/concatenate | solution.py:20
  15.4 13.7 %gather_fusion = f32[8,3,2,32,256]{3,1,2,4,0:T(4,128)} fusion(f32[8,3,2,32,512]{3,1,2,0,4:T(4,128)} %copy.169, s32[8]{0:T(128)S(1)} %fusion.100), kind=kCustom, calls=%fused_computation.clone | custom fusion | bytes 3145888 | tf_op jit(solution)/shard_map/vmap(jit(_roll_dynamic))/gather | solution.py:20
  29.1 6.4 copy.236
  35.5 7.0 copy.170
  47.7 22.4 %convolution_bitcast_fusion.2 = f32[2,6,16,8,32,16]{4,5,3,1,2,0:T(8,128)} fusion(f32[1,6,8,32,256]{4,3,0,2,1:T(8,128)S(1)} %maximum_bitcast_fusion.13, f32[1,6,8,32,256]{4,3,0,2,1:T(8,128)S(1)} %maximum_bitcast_fusion.12, f32[1,2,256,16,16]{2,4,0,3,1:T(8,128)S(1)} %get-tuple-element.72, f32[1,2,256,16,16]{2,4,0,3,1:T(8,128)S(1)} %get-tuple-element.71), kind=kOutput, calls=%fused_computation.16 | convolution fusion | flops 4832886784 | bytes 7340032 | tf_op jit(solution)/shard_map/sfabc,stcpq->tfpabq/dot_general | solution.py:34
  70.1 11.3 %fusion.116 = (f32[1,6,16,8,32,16]{4,5,3,1,2,0:T(8,128)}, f32[1,6,16,8,32,16]{4,5,3,1,2,0:T(8,128)}) fusion(f32[2,6,16,8,32,16]{4,5,3,1,2,0:T(8,128)} %convolution_bitcast_fusion.2), kind=kLoop, calls=%fused_computation.239 | loop fusion | bytes 6291456 | tf_op jit(solution)/shard_map/slice | solution.py:50
  81.4 9.7 %copy.241 = f32[1,6,16,8,32,16]{5,4,3,1,2,0:T(8,128)} copy(f32[1,6,16,8,32,16]{4,5,3,1,2,0:T(8,128)} %get-tuple-element.35) | data formatting | bytes 3145728 | tf_op jit(solution)/shard_map/reshape;squeeze | solution.py:104
  91.1 11.6 %reshape.1034 = f32[6,16,8,512]{3,2,0,1:T(8,128)} reshape(f32[1,6,16,8,32,16]{5,4,3,1,2,0:T(8,128)} %copy.241) | data formatting | bytes 3145728 | tf_op jit(solution)/shard_map/reshape;squeeze | solution.py:104
  102.6 9.5 %all-to-all-start = ((f32[6,16,8,512]{3,2,0,1:T(8,128)}), f32[6,16,8,512]{3,2,0,1:T(8,128)S(1)}, u32[]{:S(2)}, u32[]{:S(2)}) async-start(f32[6,16,8,512]{3,2,0,1:T(8,128)} %reshape.1034), calls=%async_computation | async-start | bytes 3145728 | tf_op jit(solution)/shard_map/all_to_all | solution.py:103
  112.1 9.7 %copy.242 = f32[1,6,16,8,32,16]{5,4,3,1,2,0:T(8,128)} copy(f32[1,6,16,8,32,16]{4,5,3,1,2,0:T(8,128)} %get-tuple-element.36) | data formatting | bytes 3145728 | tf_op jit(solution)/shard_map/reshape;squeeze | solution.py:107
  121.8 11.6 %reshape.1035 = f32[6,16,8,512]{3,2,0,1:T(8,128)} reshape(f32[1,6,16,8,32,16]{5,4,3,1,2,0:T(8,128)} %copy.242) | data formatting | bytes 3145728 | tf_op jit(solution)/shard_map/reshape;squeeze | solution.py:107
  134.7 5.9 all-to-all-start.1
  144.6 8.5 %stack_reshape.53 = f32[1,6,128,32,16]{4,3,2,1,0:T(8,128)} reshape(f32[6,16,8,512]{3,2,1,0:T(8,128)} %copy.189) | data formatting | bytes 3145728 | tf_op jit(solution)/shard_map/stack;reshape | solution.py:38
  153.0 9.6 %copy.193 = f32[1,6,128,32,16]{2,3,0,4,1:T(8,128)S(1)} copy(f32[1,6,128,32,16]{4,3,2,1,0:T(8,128)} %stack_reshape.53) | data formatting | bytes 3145728 | tf_op jit(solution)/shard_map/stack;reshape | solution.py:38
  164.6 8.5 %stack_reshape.54 = f32[1,6,128,32,16]{4,3,2,1,0:T(8,128)} reshape(f32[6,16,8,512]{3,2,1,0:T(8,128)} %copy.192) | data formatting | bytes 3145728 | tf_op jit(solution)/shard_map/stack;reshape | solution.py:38
  173.0 9.6 %copy.194 = f32[1,6,128,32,16]{2,3,0,4,1:T(8,128)S(1)} copy(f32[1,6,128,32,16]{4,3,2,1,0:T(8,128)} %stack_reshape.54) | data formatting | bytes 3145728 | tf_op jit(solution)/shard_map/stack;reshape | solution.py:38
  182.7 32.8 %convolution_bitcast_fusion = f32[2,6,8,32,16,32]{3,5,4,1,2,0:T(8,128)} fusion(f32[1,6,128,32,16]{2,3,0,4,1:T(8,128)S(1)} %copy.194, f32[1,6,128,32,16]{2,3,0,4,1:T(8,128)S(1)} %copy.193, f32[1,2,128,8,32]{2,4,0,3,1:T(8,128)} %get-tuple-element.76, f32[1,2,128,8,32]{2,4,0,3,1:T(8,128)S(1)} %get-tuple-element.75), kind=kOutput, calls=%fused_computation.10 | convolution fusion | flops 4832755712 | bytes 9961472 | tf_op jit(solution)/shard_map/sfkzy,stkpq->tfpzyq/dot_general | solution.py:34
  215.4 19.2 %fusion.114 = (f32[1,6,8,32,16,32]{3,5,4,1,2,0:T(8,128)}, f32[1,6,8,32,16,32]{3,5,4,1,2,0:T(8,128)}) fusion(f32[2,6,8,32,16,32]{3,5,4,1,2,0:T(8,128)} %convolution_bitcast_fusion), kind=kLoop, calls=%fused_computation.237 | loop fusion | bytes 12582912 | tf_op jit(solution)/shard_map/slice | solution.py:50
  234.6 13.3 %copy.243 = f32[1,6,8,32,16,32]{5,4,3,1,2,0:T(8,128)} copy(f32[1,6,8,32,16,32]{3,5,4,1,2,0:T(8,128)} %get-tuple-element.31) | data formatting | bytes 6291456 | tf_op jit(solution)/shard_map/reshape;squeeze | solution.py:128
  247.9 10.7 %reshape.1036 = f32[6,8,1,16384]{3,2,0,1:T(1,128)} reshape(f32[1,6,8,32,16,32]{5,4,3,1,2,0:T(8,128)} %copy.243) | data formatting | bytes 6291456 | tf_op jit(solution)/shard_map/reshape;squeeze | solution.py:128
  263.2 13.3 %copy.246 = f32[1,6,8,32,16,32]{5,4,3,1,2,0:T(8,128)} copy(f32[1,6,8,32,16,32]{3,5,4,1,2,0:T(8,128)} %get-tuple-element.32) | data formatting | bytes 6291456 | tf_op jit(solution)/shard_map/reshape;squeeze | solution.py:131
  276.4 10.6 %reshape.1038 = f32[6,8,1,16384]{3,2,0,1:T(1,128)} reshape(f32[1,6,8,32,16,32]{5,4,3,1,2,0:T(8,128)} %copy.246) | data formatting | bytes 6291456 | tf_op jit(solution)/shard_map/reshape;squeeze | solution.py:131
  287.1 20.8 %all-to-all-done.2 = f32[6,8,1,16384]{3,2,0,1:T(1,128)S(1)} async-done(((f32[6,8,1,16384]{3,2,0,1:T(1,128)}), f32[6,8,1,16384]{3,2,0,1:T(1,128)S(1)}, u32[]{:S(2)}, u32[]{:S(2)}) %all-to-all-start.2) | async-done | bytes 3145760 | tf_op jit(solution)/shard_map/all_to_all | solution.py:127
  316.4 10.8 %reduce.1 = f32[6,8,16384]{2,0,1:T(8,128)} reduce(f32[6,8,1,16384]{3,2,0,1:T(1,128)S(1)} %all-to-all-done.2, f32[]{:T(128)} %constant.214), dimensions={2}, to_apply=%all_to_all.18.reduce_sub_computation | reduce | bytes 6291460 | tf_op jit(solution)/shard_map/all_to_all | solution.py:127
  327.1 9.7 %reshape.1037 = f32[1,6,8,32,16,32]{5,4,3,1,2,0:T(8,128)} reshape(f32[6,8,16384]{2,0,1:T(8,128)} %reduce.1) | data formatting | bytes 6291456 | tf_op jit(solution)/shard_map/stack;reshape | solution.py:136
  336.9 13.0 %copy.201 = f32[1,6,8,32,16,32]{3,5,0,2,4,1:T(8,128)} copy(f32[1,6,8,32,16,32]{5,4,3,1,2,0:T(8,128)} %reshape.1037) | data formatting | bytes 6291456 | tf_op jit(solution)/shard_map/stack;reshape | solution.py:136
  349.9 7.1 %all-to-all-done.3 = f32[6,8,1,16384]{3,2,0,1:T(1,128)} async-done(((f32[6,8,1,16384]{3,2,0,1:T(1,128)}), f32[6,8,1,16384]{3,2,0,1:T(1,128)}, u32[]{:S(2)}, u32[]{:S(2)}) %all-to-all-start.3) | async-done | bytes 3145760 | tf_op jit(solution)/shard_map/all_to_all | solution.py:130
  357.0 11.7 %reduce.2 = f32[6,8,16384]{2,0,1:T(8,128)} reduce(f32[6,8,1,16384]{3,2,0,1:T(1,128)} %all-to-all-done.3, f32[]{:T(128)} %constant.214), dimensions={2}, to_apply=%all_to_all.19.reduce_sub_computation | reduce | bytes 6291460 | tf_op jit(solution)/shard_map/all_to_all | solution.py:130
  368.7 9.7 %reshape.1039 = f32[1,6,8,32,16,32]{5,4,3,1,2,0:T(8,128)} reshape(f32[6,8,16384]{2,0,1:T(8,128)} %reduce.2) | data formatting | bytes 6291456 | tf_op jit(solution)/shard_map/stack;reshape | solution.py:136
  378.4 12.9 %copy.202 = f32[1,6,8,32,16,32]{3,5,0,2,4,1:T(8,128)} copy(f32[1,6,8,32,16,32]{5,4,3,1,2,0:T(8,128)} %reshape.1039) | data formatting | bytes 6291456 | tf_op jit(solution)/shard_map/stack;reshape | solution.py:136
  391.3 24.4 %fusion.17 = f32[6,16,32,256]{3,2,1,0:T(8,128)S(1)} fusion(f32[1,6,8,32,16,32]{3,5,0,2,4,1:T(8,128)} %copy.202, f32[1,6,8,32,16,32]{3,5,0,2,4,1:T(8,128)} %copy.201, f32[1,8,32,256]{3,2,0,1:T(8,128)S(1)} %copy-done.17, f32[1,8,32,256]{3,2,0,1:T(8,128)S(1)} %copy-done.16), kind=kOutput, calls=%fused_computation.29 | convolution fusion | flops 4833542144 | bytes 9961472 | tf_op jit(solution)/shard_map/sfpkyq,spkn->fyqn/dot_general | solution.py:34
  416.6 12.6 %convolution_bitcast_fusion.1 = f32[2,3,8,32,16,32]{5,3,4,1,2,0:T(8,128)} fusion(f32[1,16,32,256]{3,2,1,0:T(8,128)S(1)} %get-tuple-element.41, f32[1,16,32,256]{3,2,1,0:T(8,128)S(1)} %get-tuple-element.40, f32[1,16,32,256]{3,2,1,0:T(8,128)S(1)} %get-tuple-element.39, f32[1,256,8,32]{1,3,2,0:T(8,128)S(1)} %copy-done.9, ...), kind=kOutput, calls=%fused_computation.15 | convolution fusion | flops 2416836608 | bytes 5242880 | tf_op jit(solution)/shard_map/fyqn,tnpk->tfpkyq/dot_general | solution.py:34
  429.2 9.2 %fusion.115 = (f32[1,3,8,32,16,32]{5,3,4,1,2,0:T(8,128)S(1)}, f32[1,3,8,32,16,32]{5,3,4,1,2,0:T(8,128)}) fusion(f32[2,3,8,32,16,32]{5,3,4,1,2,0:T(8,128)} %convolution_bitcast_fusion.1), kind=kLoop, calls=%fused_computation.238 | loop fusion | bytes 6291456 | tf_op jit(solution)/shard_map/slice | solution.py:152
  438.4 8.1 %copy.249 = f32[1,3,8,32,16,32]{5,4,3,1,2,0:T(8,128)} copy(f32[1,3,8,32,16,32]{5,3,4,1,2,0:T(8,128)S(1)} %get-tuple-element.33) | data formatting | bytes 3145728 | tf_op jit(solution)/shard_map/reshape;squeeze | solution.py:156
  446.4 6.0 reshape.1040
  456.2 10.9 %copy.252 = f32[1,3,8,32,16,32]{5,4,3,1,2,0:T(8,128)} copy(f32[1,3,8,32,16,32]{5,3,4,1,2,0:T(8,128)} %get-tuple-element.34) | data formatting | bytes 3145728 | tf_op jit(solution)/shard_map/reshape;squeeze | solution.py:159
  467.1 5.9 reshape.1042
  495.7 7.4 %copy.209 = f32[1,3,8,32,16,32]{5,3,0,2,4,1:T(8,128)} copy(f32[1,3,8,32,16,32]{5,4,3,1,2,0:T(8,128)} %reshape.1041) | data formatting | bytes 3145728 | tf_op jit(solution)/shard_map/stack;reshape | solution.py:38
  519.1 41.8 %fusion.14 = f32[2,3,16,8,32,16]{4,2,5,1,3,0:T(8,128)S(1)} fusion(f32[1,3,8,32,16,32]{5,3,0,2,4,1:T(8,128)S(1)} %copy.210, f32[1,3,8,32,16,32]{5,3,0,2,4,1:T(8,128)} %copy.209, f32[2,2,8,32,16,8,1,1]{3,4,0,2,7,6,5,1:T(8,128)S(1)} %copy-done.7), kind=kOutput, calls=%fused_computation.25 | convolution fusion | flops 2416705536 | bytes 5242880 | tf_op jit(solution)/shard_map/sfpkyq,stpqmr->tfmrky/dot_general | solution.py:34
  563.3 5.9 copy.255
  574.6 9.6 %all-to-all-start.6 = ((f32[3,16,1,4096]{3,2,0,1:T(1,128)}), f32[3,16,1,4096]{3,2,0,1:T(1,128)}, u32[]{:S(2)}, u32[]{:S(2)}) async-start(f32[3,16,1,4096]{3,2,0,1:T(1,128)} %reshape.1044), calls=%async_computation.6 | async-start | bytes 1572864 | tf_op jit(solution)/shard_map/all_to_all | solution.py:176
  604.8 12.1 %copy.172 = f32[8,3,2,32,512]{3,1,2,0,4:T(4,128)} copy(f32[8,3,2,32,512]{4,3,2,1,0:T(8,128)S(1)} %pad_maximum_fusion.1) | data formatting | bytes 6291456 | tf_op jit(solution)/shard_map/vmap(jit(_roll_dynamic))/concatenate | solution.py:20
  616.9 13.7 %gather_fusion.1 = f32[8,3,2,32,256]{3,1,2,4,0:T(4,128)} fusion(f32[8,3,2,32,512]{3,1,2,0,4:T(4,128)} %copy.172, s32[8]{0:T(128)S(1)} %copy-done.21), kind=kCustom, calls=%fused_computation.1.clone | custom fusion | bytes 3145888 | tf_op jit(solution)/shard_map/vmap(jit(_roll_dynamic))/gather | solution.py:20
  630.6 6.5 copy.173
  649.8 6.1 copy.217
  665.5 6.2 copy.218
  671.6 13.9 %fusion.25 = f32[2,3,8,32,256]{4,3,2,1,0:T(8,128)S(1)} fusion(f32[1,3,16,8,32,16]{4,5,0,2,3,1:T(8,128)} %copy.218, f32[1,3,16,8,32,16]{4,5,0,2,3,1:T(8,128)} %copy.217, f32[1,2,16,16,256]{4,3,0,2,1:T(8,128)} %get-tuple-element.70, f32[1,2,16,16,256]{4,3,0,2,1:T(8,128)} %get-tuple-element.69), kind=kOutput, calls=%fused_computation.43 | convolution fusion | flops 2416574464 | bytes 4194304 | tf_op jit(solution)/shard_map/sfparq,stpqn->tfarn/dot_general | solution.py:34
  689.7 14.4 %all-reduce = (f32[8]{0:T(128)S(1)}, f32[8]{0:T(128)S(1)}) all-reduce(f32[8]{0:T(128)S(1)} %multiply_reduce_fusion.1, f32[8]{0:T(128)S(1)} %add_reduce_fusion), channel_id=1, replica_groups=mesh['row'=16,'col'=8] {'col'}, use_global_device_ids=true, to_apply=%region_4.6 | all-reduce | flops 16 | bytes 128 | tf_op jit(solution)/shard_map/psum | solution.py:235
  (151 shorter events, 127.7 us)
Async XLA Ops:
  0.7 44.8 %copy-start.29 = (f32[8]{0:T(128)}, f32[8]{0:T(128)S(1)}, u32[]{:S(2)}) copy-start(f32[8]{0:T(128)S(1)} %fusion.101) | copy-start | bytes 100
  0.7 44.8 %copy-start.24 = (f32[32]{0:T(128)}, f32[32]{0:T(128)S(1)}, u32[]{:S(2)}) copy-start(f32[32]{0:T(128)S(1)} %fusion.102) | copy-start | bytes 388
  0.7 43.8 %copy-start.26 = (f32[32]{0:T(128)}, f32[32]{0:T(128)S(1)}, u32[]{:S(2)}) copy-start(f32[32]{0:T(128)S(1)} %fusion.109) | copy-start | bytes 388
  2.6 12.1 %copy-start.31 = (s32[8]{0:T(128)S(1)}, s32[8]{0:T(128)}, u32[]{:S(2)}) copy-start(s32[8]{0:T(128)} %param.12) | copy-start | bytes 100
  2.7 12.1 %copy-start.32 = (s32[8]{0:T(128)S(1)}, s32[8]{0:T(128)}, u32[]{:S(2)}) copy-start(s32[8]{0:T(128)} %param.13) | copy-start | bytes 100
  14.8 0.6 copy-start.20
  35.5 9.4 %copy-start = (f32[8,3,2,32,256]{4,3,0,2,1:T(8,128)}, f32[8,3,2,32,256]{4,3,0,2,1:T(8,128)S(1)}, u32[]{:S(2)}) copy-start(f32[8,3,2,32,256]{4,3,0,2,1:T(8,128)S(1)} %copy.236) | copy-start | bytes 4718596
  42.5 3.0 copy-start.2
  42.6 3.7 copy-start.22
  44.6 0.9 copy-start.18
  44.6 1.0 copy-start.14
  45.3 0.7 copy-start.5
  102.6 32.1 %all-to-all-start = ((f32[6,16,8,512]{3,2,0,1:T(8,128)}), f32[6,16,8,512]{3,2,0,1:T(8,128)S(1)}, u32[]{:S(2)}, u32[]{:S(2)}) async-start(f32[6,16,8,512]{3,2,0,1:T(8,128)} %reshape.1034), calls=%async_computation | async-start | bytes 3145728 | tf_op jit(solution)/shard_map/all_to_all | solution.py:103
  134.7 28.6 %all-to-all-start.1 = ((f32[6,16,8,512]{3,2,0,1:T(8,128)}), f32[6,16,8,512]{3,2,0,1:T(8,128)S(1)}, u32[]{:S(2)}, u32[]{:S(2)}) async-start(f32[6,16,8,512]{3,2,0,1:T(8,128)} %reshape.1035), calls=%async_computation.1 | async-start | bytes 3145728 | tf_op jit(solution)/shard_map/all_to_all | solution.py:106
  141.7 0.7 copy-start.10
  141.7 0.8 copy-start.12
  258.5 49.4 %all-to-all-start.2 = ((f32[6,8,1,16384]{3,2,0,1:T(1,128)}), f32[6,8,1,16384]{3,2,0,1:T(1,128)S(1)}, u32[]{:S(2)}, u32[]{:S(2)}) async-start(f32[6,8,1,16384]{3,2,0,1:T(1,128)} %reshape.1036), calls=%async_computation.2 | async-start | bytes 6291456 | tf_op jit(solution)/shard_map/all_to_all | solution.py:127
  307.9 49.2 %all-to-all-start.3 = ((f32[6,8,1,16384]{3,2,0,1:T(1,128)}), f32[6,8,1,16384]{3,2,0,1:T(1,128)}, u32[]{:S(2)}, u32[]{:S(2)}) async-start(f32[6,8,1,16384]{3,2,0,1:T(1,128)} %reshape.1038), calls=%async_computation.3 | async-start | bytes 6291456 | tf_op jit(solution)/shard_map/all_to_all | solution.py:130
  378.4 12.9 %copy-start.16 = (f32[1,8,32,256]{3,2,0,1:T(8,128)S(1)}, f32[1,8,32,256]{3,2,0,1:T(8,128)}, u32[]{:S(2)}) copy-start(f32[1,8,32,256]{3,2,0,1:T(8,128)} %get-tuple-element.88) | copy-start | bytes 786436
  378.4 12.9 %copy-start.17 = (f32[1,8,32,256]{3,2,0,1:T(8,128)S(1)}, f32[1,8,32,256]{3,2,0,1:T(8,128)}, u32[]{:S(2)}) copy-start(f32[1,8,32,256]{3,2,0,1:T(8,128)} %get-tuple-element.89) | copy-start | bytes 786436
  415.7 1.0 copy-start.9
  452.4 25.5 %all-to-all-start.4 = ((f32[3,8,1,16384]{3,2,0,1:T(1,128)}), f32[3,8,1,16384]{3,2,0,1:T(1,128)S(1)}, u32[]{:S(2)}, u32[]{:S(2)}) async-start(f32[3,8,1,16384]{3,2,0,1:T(1,128)} %reshape.1040), calls=%async_computation.4 | async-start | bytes 3145728 | tf_op jit(solution)/shard_map/all_to_all | solution.py:155
  473.0 9.5 %copy-start.13 = (f32[256,256]{0,1:T(8,128)S(1)}, f32[256,256]{0,1:T(8,128)}, u32[]{:S(2)}) copy-start(f32[256,256]{0,1:T(8,128)} %copy-done.12) | copy-start | bytes 786436
  473.0 9.5 %copy-start.11 = (f32[256,256]{0,1:T(8,128)S(1)}, f32[256,256]{0,1:T(8,128)}, u32[]{:S(2)}) copy-start(f32[256,256]{0,1:T(8,128)} %copy-done.10) | copy-start | bytes 786436
  477.9 5.6 copy-start.4
  477.9 26.2 %all-to-all-start.5 = ((f32[3,8,1,16384]{3,2,0,1:T(1,128)}), f32[3,8,1,16384]{3,2,0,1:T(1,128)}, u32[]{:S(2)}, u32[]{:S(2)}) async-start(f32[3,8,1,16384]{3,2,0,1:T(1,128)} %reshape.1042), calls=%async_computation.5 | async-start | bytes 3145728 | tf_op jit(solution)/shard_map/all_to_all | solution.py:158
  514.1 5.0 copy-start.7
  574.6 23.3 %all-to-all-start.6 = ((f32[3,16,1,4096]{3,2,0,1:T(1,128)}), f32[3,16,1,4096]{3,2,0,1:T(1,128)}, u32[]{:S(2)}, u32[]{:S(2)}) async-start(f32[3,16,1,4096]{3,2,0,1:T(1,128)} %reshape.1044), calls=%async_computation.6 | async-start | bytes 1572864 | tf_op jit(solution)/shard_map/all_to_all | solution.py:176
  588.4 15.8 %copy-start.8 = (f32[3,2,8,32,256]{4,3,2,1,0:T(8,128)S(1)}, f32[3,2,8,32,256]{4,3,2,1,0:T(8,128)}, u32[]{:S(2)}) copy-start(f32[3,2,8,32,256]{4,3,2,1,0:T(8,128)} %param.11) | copy-start | bytes 4718596
  597.9 58.0 %all-to-all-start.7 = ((f32[3,16,1,4096]{3,2,0,1:T(1,128)}), f32[3,16,1,4096]{3,2,0,1:T(1,128)}, u32[]{:S(2)}, u32[]{:S(2)}) async-start(f32[3,16,1,4096]{3,2,0,1:T(1,128)} %reshape.1046), calls=%async_computation.7 | async-start | bytes 1572864 | tf_op jit(solution)/shard_map/all_to_all | solution.py:179
  604.7 12.1 %copy-start.21 = (s32[8]{0:T(128)S(1)}, s32[8]{0:T(128)}, u32[]{:S(2)}) copy-start(s32[8]{0:T(128)} %copy-done.20) | copy-start | bytes 100
  630.6 7.2 %copy-start.1 = (f32[8,3,2,32,256]{4,3,0,2,1:T(8,128)S(1)}, f32[8,3,2,32,256]{4,3,0,2,1:T(8,128)}, u32[]{:S(2)}) copy-start(f32[8,3,2,32,256]{4,3,0,2,1:T(8,128)} %copy-done) | copy-start | bytes 4718596
  630.6 7.4 %copy-start.23 = (s32[16,16]{1,0:T(8,128)S(1)}, s32[16,16]{1,0:T(8,128)}, u32[]{:S(2)}) copy-start(s32[16,16]{1,0:T(8,128)} %copy-done.22) | copy-start | bytes 3076
  671.6 13.9 %copy-start.6 = (f32[8,32,256]{2,1,0:T(8,128)S(1)}, f32[8,32,256]{2,1,0:T(8,128)}, u32[]{:S(2)}) copy-start(f32[8,32,256]{2,1,0:T(8,128)} %copy-done.5) | copy-start | bytes 786436
  685.5 0.7 copy-start.15
  685.5 0.7 copy-start.19
  685.5 0.7 copy-start.25
  685.6 0.7 copy-start.27
  685.6 0.7 copy-start.28
  685.6 0.7 copy-start.30
  685.6 1.4 copy-start.3
where the time goes:
time: 721 us; the launch traced here: 709 us
  local copies, waits for them, and re-layouts  393 us (55%)
  matrix products  148 us (21%)
  other arithmetic  61.2 us (8%)
  starting transfers between devices  48.2 us (7%)
  waiting for transfers between devices  39.9 us (6%)
  blocking collectives  14.4 us (2%)
    dot_general x6, matrix products, product_high(): jnp.einsum(formula, first_arg, second_arg, precision=lax.Precision.HIGHEST)  148 us
    another operation x12, local copies, waits for them, and re-layouts, rotate(): stacked = jnp.stack([real_part, imag_part])  80.2 us
    another operation x4, local copies, waits for them, and re-layouts, to_physical(): jnp.stack([fourth_real.reshape(deep_shape), fourth_imag.reshape(deep_shap...  45.3 us
    gather x4, local copies, waits for them, and re-layouts, shift_row(): return jnp.roll(row_data, -amount_one, axis=-1)  40.9 us
    slice x3, local copies, waits for them, and re-layouts, rotate(): return (result[0], result[1])  32.8 us
    concatenate x2, local copies, waits for them, and re-layouts, shift_row(): return jnp.roll(row_data, -amount_one, axis=-1)  24.2 us
    another operation x2, local copies, waits for them, and re-layouts, to_physical(): third_real.reshape(flat_shape)  23.9 us
    another operation x2, local copies, waits for them, and re-layouts, to_physical(): third_imag.reshape(flat_shape)  23.9 us
  transfers between devices with their start and end apart: 8, of which 7 were waited for; matrix products, arithmetic and copies ran while one was open for 28% of the time, Pallas kernels for 0%

commit v1 on v0

v1 whole, which is shorter than its diff:
```python
import numpy as np
import jax
import jax.numpy as jnp
from jax import lax
from jax.experimental import pallas as pl
from jax.experimental.pallas import tpu as pltpu
from jax.sharding import PartitionSpec as P

N = 256
ROWS = 11
F32 = jnp.float32
BF16 = jnp.bfloat16
VLIM = 60 * 1024 * 1024


def halves(table):
    table = table.astype(np.float32)
    high = table.astype(jnp.bfloat16)
    low = (table - high.astype(np.float32)).astype(jnp.bfloat16)
    return np.stack([high, low])


def tables():
    index = np.arange(N)
    angle = (index[:, None] * index[None, :] % N) * (2.0 * np.pi / N)
    cos, sin = np.cos(angle) / 16.0, np.sin(angle) / 16.0
    first = np.block([[cos, -sin], [sin, cos]])
    second = np.block([[cos, sin], [-sin, cos]])
    count = ROWS * 8
    weights = np.where(np.arange(count) == 0, 1.0, 2.0)
    back_x = np.concatenate([cos[:, :count] * weights, -sin[:, :count] * weights], axis=1)
    fore_x = np.concatenate([cos[:count], -sin[:count]], axis=0)
    return halves(first), halves(second), halves(back_x), halves(fore_x)


def split(value):
    high = value.astype(BF16)
    return high, (value - high.astype(F32)).astype(BF16)


def dot3(left, right, dims=((1,), (0,))):
    def one(a, b):
        return lax.dot_general(a, b, (dims, ((), ())), preferred_element_type=F32)

    return one(left[0], right[0]) + one(left[1], right[0]) + one(left[0], right[1])


def swap_chunks(items, width):
    items = list(items)
    count = len(items)
    lane = lax.broadcasted_iota(jnp.int32, items[0].shape, items[0].ndim - 1) // width
    axis = items[0].ndim - 1
    step = count // 2
    while step:
        keep = (lane & step) == 0
        for i in range(count):
            if i & step == 0:
                a, b = items[i], items[i + step]
                items[i] = jnp.where(keep, a, pltpu.roll(b, step * width, axis))
                items[i + step] = jnp.where(keep, pltpu.roll(a, 128 - step * width, axis), b)
        step //= 2
    return items


def swap_wide(items):
    out = [[None, None] for _ in range(8)]
    for g in range(2):
        for h in range(2):
            part = swap_chunks([items[4 * g + i][:, 128 * h:128 * h + 128] for i in range(4)], 32)
            for j in range(4):
                out[4 * h + j][g] = part[j]
    return [jnp.concatenate(pair, axis=1) for pair in out]


def signed(index):
    return jnp.where(2 * index < N, index, index - N)


def modes(kx_index, kz_index, ky_index, drift):
    wave_x = kx_index.astype(F32)
    wave_z = signed(kz_index).astype(F32)
    wave_y = signed(ky_index).astype(F32) - drift * wave_x
    square = wave_x * wave_x + wave_y * wave_y + wave_z * wave_z
    mask = (3 * kx_index < N) & (3 * jnp.abs(signed(kz_index)) < N) & (3 * jnp.abs(signed(ky_index)) < N)
    return wave_x, wave_y, wave_z, square, mask


def joined(data):
    return jnp.concatenate([data[g] for g in range(4)], axis=1)


def pre_kernel(place, offset, scal, velocity, high_out, low_out, sums_out):
    step = pl.program_id(0)
    shift = (0 - offset[step]) & (N - 1)
    kx = jnp.full((32, N), place[0] * 8 + step, jnp.int32)
    kz = lax.broadcasted_iota(jnp.int32, (32, N), 0) + place[1] * 32
    ky = lax.broadcasted_iota(jnp.int32, (32, N), 1)
    wave_x, wave_y, wave_z, square, mask = modes(kx, kz, ky, scal[1] * scal[2])
    inverse = 1.0 / jnp.maximum(square, 1.0)
    wave = (wave_x, wave_y, wave_z)
    energy = jnp.zeros((32, N), F32)
    stress = jnp.zeros((32, N), F32)
    for p in range(2):
        v = [pltpu.roll(velocity[c, p, 0], shift, 1) for c in range(3)]
        energy += v[0] * v[0] + v[1] * v[1] + v[2] * v[2]
        stress += v[0] * v[1]
        along = (wave[0] * v[0] + wave[1] * v[1] + wave[2] * v[2]) * inverse
        for c in range(3):
            high, low = split(jnp.where(mask, v[c] - wave[c] * along, 0.0))
            high_out[c, :, p * N:(p + 1) * N] = high
            low_out[c, :, p * N:(p + 1) * N] = low
    def total(value):
        value = jnp.sum(value, axis=0, keepdims=True)
        return value[:, :128] + value[:, 128:]
    sums_out[0, 0:1, :] = total(stress)
    sums_out[0, 1:2, :] = total(square * energy)


def y_back(high, low, first, out):
    result = dot3((first[0], first[1]), (high[0], low[0]), ((1,), (1,)))
    for c in range(8):
        for p in range(2):
            out[c, 0, p] = result[p * N + 32 * c:p * N + 32 * c + 32]


def z_back(block, second, out, data):
    for p in range(2):
        moved = swap_wide([block[s, 0, p] for s in range(8)])
        for kx in range(8):
            for g in range(2):
                data[2 * p + g, pl.ds(kx, 32, stride=8), :] = moved[kx][:, 128 * g:128 * g + 128]
    result = dot3(split(joined(data)), (second[0], second[1])).reshape(4, 8, 8, 2 * N)
    for p in range(2):
        for h in range(2):
            lanes = slice(p * N + 128 * h, p * N + 128 * h + 128)
            moved = swap_chunks([result[:, i, :, lanes] for i in range(8)], 16)
            for r in range(8):
                for j in range(4):
                    out[8 * h + r, 0, p, :, 128 * j:128 * j + 128] = moved[r][j]


def x_both(block, back, fore, out):
    lanes = block.shape[-1]
    count = ROWS * 8
    u = []
    for c in range(3):
        both = jnp.concatenate([block[:ROWS, c, p].reshape(count, lanes) for p in range(2)], axis=0)
        u.append(dot3((back[0], back[1]), split(both)))
    square = u[0] * u[0]
    fields = [u[0] * u[1], u[0] * u[2], u[1] * u[2], u[1] * u[1] - square, u[2] * u[2] - square]
    for t in range(5):
        hat = dot3((fore[0], fore[1]), split(fields[t])).reshape(2, ROWS, 8, lanes)
        for p in range(2):
            for r in range(ROWS):
                out[r, t, p] = hat[p, r]
            for r in range(ROWS, 16):
                out[r, t, p] = jnp.zeros((8, lanes), F32)


def z_fore(place, block, first, out, data, hats):
    for t in range(5):
        for p in range(2):
            for h in range(2):
                for j in range(4):
                    moved = swap_chunks([block[8 * h + s, t, p, :, 128 * j:128 * j + 128] for s in range(8)], 16)
                    for i in range(8):
                        data[2 * p + h, (8 * j + i) * 8:(8 * j + i) * 8 + 8, :] = moved[i]
        hats[t] = dot3(split(joined(data)), (first[0], first[1]))
    kx_index = (lax.broadcasted_iota(jnp.int32, (N, N), 0) & 7) + place[0] * 8
    kz_index = lax.broadcasted_iota(jnp.int32, (N, N), 1)
    kx = kx_index.astype(F32)
    kz = signed(kz_index).astype(F32)
    origin = (kx_index == 0) & (kz_index == 0)
    for p in range(2):
        t01, t02, t12, t11, t22 = [hats[t, :, p * N:(p + 1) * N] for t in range(5)]
        cross = kx * kz
        fields = [
            jnp.where(origin, t01, kx * t01 + kz * t12),
            2.0 * cross * t02 + kz * kz * t22 - (kx * kx + kz * kz) * t11,
            (kz * kz - kx * kx) * t02 - cross * t22,
            jnp.where(origin, t12, kz * t01 - kx * t12),
        ]
        for g in range(4):
            for h in range(2):
                data[h] = fields[g][:, 128 * h:128 * h + 128]
            moved = swap_wide([jnp.concatenate([data[h, pl.ds(i, 32, stride=8), :] for h in range(2)], axis=1) for i in range(8)])
            for c in range(8):
                out[c, g, p] = moved[c]


def post_kernel(place, offset, scal, block, second, velocity, accumulator, new_velocity, new_accumulator):
    step = pl.program_id(0)
    drift = scal[1] * scal[2]
    hats = []
    for g in range(4):
        both = jnp.concatenate([block[:, g, p].reshape(N, 128) for p in range(2)], axis=0)
        result = dot3((second[0], second[1]), split(both))
        hats.append((result[:N], result[N:]))
    lane = lax.broadcasted_iota(jnp.int32, (N, 128), 1)
    kx_index = lane // 32 + (place[0] * 8 + step * 4)
    kz_index = lane % 32 + place[1] * 32
    ky_index = lax.broadcasted_iota(jnp.int32, (N, 128), 0)
    kx, k1, kz, square, mask = modes(kx_index, kz_index, ky_index, drift)
    flat = kx * kx + kz * kz
    origin = flat == 0.0
    over_square = 1.0 / jnp.maximum(square, 1.0)
    over_flat = 1.0 / jnp.maximum(flat, 1.0)
    result = [[None, None] for _ in range(3)]
    for p in range(2):
        sign = -1.0 if p == 0 else 1.0
        x, q, r, s = [sign * hats[g][1 - p] for g in range(4)]
        v = ((k1 * k1 - flat) * x + k1 * q) * over_square
        w = 0.0 - (r + k1 * s)
        part = [
            jnp.where(origin, 0.0 - k1 * x, (kz * w - kx * k1 * v) * over_flat),
            jnp.where(origin, 0.0, v),
            jnp.where(origin, 0.0 - k1 * s, (0.0 - kx * w - kz * k1 * v) * over_flat),
        ]
        for c in range(3):
            result[c][p] = jnp.where(mask, part[c], 0.0).T
    for i in range(4):
        shift = (0 - offset[step * 4 + i]) & (N - 1)
        kx_index = jnp.full((32, N), place[0] * 8 + step * 4 + i, jnp.int32)
        kz_index = lax.broadcasted_iota(jnp.int32, (32, N), 0) + place[1] * 32
        ky_index = lax.broadcasted_iota(jnp.int32, (32, N), 1)
        kx, k1, kz, square, _ = modes(kx_index, kz_index, ky_index, drift)
        wave = (kx, k1, kz)
        coupling = 2.0 * scal[1] * kx / jnp.maximum(square, 1.0)
        damp = scal[0] * square
        for p in range(2):
            v = [pltpu.roll(velocity[c, p, i], shift, 1) for c in range(3)]
            for c in range(3):
                rate = result[c][p][32 * i:32 * i + 32] + coupling * wave[c] * v[1] - damp * v[c]
                if c == 0:
                    rate = rate - scal[1] * v[1]
                fresh = (-5.0 / 9.0) * pltpu.roll(accumulator[c, p, i], shift, 1) + scal[3] * rate
                new_accumulator[c, p, i] = fresh
                new_velocity[c, p, i] = v[c] + (15.0 / 16.0) * fresh


def call(kernel, grid, ins, outs, scratch=()):
    return pl.pallas_call(
        kernel,
        grid=grid,
        in_specs=ins,
        out_specs=[spec for spec, _ in outs],
        out_shape=[shape for _, shape in outs],
        scratch_shapes=list(scratch),
        compiler_params=pltpu.CompilerParams(vmem_limit_bytes=VLIM),
    )


def spec(shape, index):
    return pl.BlockSpec(shape, index)


def whole(array):
    rank = array.ndim
    return pl.BlockSpec(array.shape, lambda *_: (0,) * rank)


SMEM = pl.BlockSpec(memory_space=pltpu.SMEM)


def exchange(value, axis):
    return lax.all_to_all(value, axis, split_axis=0, concat_axis=0, tiled=True)


def body(velocity, accumulator, remesh_flag, remesh_shift, viscosity, shear, clock, step):
    first, second, back, fore = [jnp.asarray(table) for table in tables()]
    place = jnp.stack([lax.axis_index("row"), lax.axis_index("col")]).astype(jnp.int32)
    offset = remesh_flag * remesh_shift
    scal = jnp.concatenate([viscosity, shear, clock, step])
    shape = jax.ShapeDtypeStruct
    high, low, sums = call(
        pre_kernel, (8,),
        [SMEM, SMEM, SMEM, spec((3, 2, 1, 32, N), lambda i: (0, 0, i, 0, 0))],
        [(spec((3, 32, 2 * N), lambda i: (0, i, 0)), shape((3, N, 2 * N), BF16)),
         (spec((3, 32, 2 * N), lambda i: (0, i, 0)), shape((3, N, 2 * N), BF16)),
         (spec((1, 8, 128), lambda i: (i, 0, 0)), shape((8, 8, 128), F32))],
    )(place, offset, scal, velocity)
    [one] = call(
        y_back, (3,),
        [spec((1, N, 2 * N), lambda f: (f, 0, 0)), spec((1, N, 2 * N), lambda f: (f, 0, 0)), whole(first)],
        [(spec((8, 1, 2, 32, N), lambda f: (0, f, 0, 0, 0)), shape((8, 3, 2, 32, N), F32))],
    )(high, low, first)
    one = exchange(one, "col")
    [two] = call(
        z_back, (3,),
        [spec((8, 1, 2, 32, N), lambda f: (0, f, 0, 0, 0)), whole(second)],
        [(spec((16, 1, 2, 8, 2 * N), lambda f: (0, f, 0, 0, 0)), shape((16, 3, 2, 8, 2 * N), F32))],
        [pltpu.VMEM((4, N, 128), F32)],
    )(one, second)
    two = exchange(two, "row")
    [three] = call(
        x_both, (2,),
        [spec((16, 3, 2, 8, N), lambda i: (0, 0, 0, 0, i)), whole(back), whole(fore)],
        [(spec((16, 5, 2, 8, N), lambda i: (0, 0, 0, 0, i)), shape((16, 5, 2, 8, 2 * N), F32))],
    )(two, back, fore)
    three = exchange(three, "row")
    [four] = call(
        z_fore, (1,),
        [SMEM, whole(three), whole(first)],
        [(spec((8, 4, 2, 32, N), lambda i: (0, 0, 0, 0, 0)), shape((8, 4, 2, 32, N), F32))],
        [pltpu.VMEM((4, N, 128), F32), pltpu.VMEM((5, N, 2 * N), F32)],
    )(place, three, first)
    four = exchange(four, "col")
    state = spec((3, 2, 4, 32, N), lambda i: (0, 0, i, 0, 0))
    new_velocity, new_accumulator = call(
        post_kernel, (2,),
        [SMEM, SMEM, SMEM, spec((8, 4, 2, 32, 128), lambda i: (0, 0, 0, 0, i)), whole(second), state, state],
        [(state, shape(velocity.shape, F32)), (state, shape(velocity.shape, F32))],
    )(place, offset, scal, four, second, velocity, accumulator)
    total = lax.psum(jnp.sum(sums[:, :2], axis=2), "col")
    scale = jnp.stack([jnp.ones((), F32), 2.0 * viscosity[0]]) / (N * N)
    return new_velocity, new_accumulator, total.T * scale[:, None]


def solution(mesh):
    state = P(None, None, "row", "col", None)
    return jax.shard_map(
        body,
        mesh=mesh,
        in_specs=(state, state, P("row"), P("row"), P(), P(), P(), P()),
        out_specs=(state, state, P(None, "row")),
        check_vma=False,
    )
```

time: 721 us -> 195 us (0.27); the launches traced: 709 us -> 191 us
  local copies, waits for them, and re-layouts: 393 us -> 1.99 us
  matrix products: 148 us -> 0 us
  blocking collectives: 14.4 us -> 132 us
  other arithmetic: 61.2 us -> 3.38 us
  Pallas kernels: 0 us -> 47.1 us
  starting transfers between devices: 48.2 us -> 3.6 us
  waiting for transfers between devices: 39.9 us -> 0.01 us
    another operation x34 -> x0, local copies, waits for them, and re-layouts: 268 us -> none  [the longest x12 80.2 us: rotate(): stacked = jnp.stack([real_part, imag_part])]
    dot_general x6 -> x0, matrix products: 148 us -> none  [product_high(): jnp.einsum(formula, first_arg, second_arg, precision=lax.Precision.HIGHEST)]
    all_to_all x0 -> x3, blocking collectives: none -> 97.5 us  [exchange(): return lax.all_to_all(value, axis, split_axis=0, concat_axis=0, tiled=True)]
    pallas_call x0 -> x6, Pallas kernels: none -> 47.1 us  [the longest x1 18.5 us: body(): call(z_fore, (1,), [SMEM, whole(three), whole(first)], [(spec((8, 4, 2, 3...]
    all_to_all x8 -> x1, starting transfers between devices: 48.2 us -> 3.6 us  [exchange(): return lax.all_to_all(value, axis, split_axis=0, concat_axis=0, tiled=True)]
    all_to_all x6 -> x0, other arithmetic: 42.5 us -> none  [the longest x1 11.7 us: to_physical(): lax.all_to_all(third_imag.reshape(flat_shape), 'col', split_axis=1, conca...]
    slice x6 -> x0, local copies, waits for them, and re-layouts: 42 us -> none  [the longest x3 32.8 us: rotate(): return (result[0], result[1])]
    gather x4 -> x0, local copies, waits for them, and re-layouts: 40.9 us -> none  [shift_row(): return jnp.roll(row_data, -amount_one, axis=-1)]
  transfers between devices with their start and end apart: 8 -> 1, of which waited for: 7 -> 0; matrix products, arithmetic and copies ran while one was open for 28% -> 1% of each run, Pallas kernels for 0% -> 0%
where the time goes in v1:
time: 195 us; the launch traced here: 191 us
  blocking collectives  132 us (68%)
  Pallas kernels  47.1 us (24%)
  starting transfers between devices  3.6 us (2%)
  other arithmetic  3.38 us (2%)
  between operations  3.24 us (2%)
  local copies, waits for them, and re-layouts  1.99 us (1%)
    all_to_all x3, blocking collectives, exchange(): return lax.all_to_all(value, axis, split_axis=0, concat_axis=0, tiled=True)  97.5 us
    psum x1, blocking collectives, body(): total = lax.psum(jnp.sum(sums[:, :2], axis=2), 'col')  34.4 us
    pallas_call x1, Pallas kernels, body(): call(z_fore, (1,), [SMEM, whole(three), whole(first)], [(spec((8, 4, 2, 3...  18.5 us
    pallas_call x1, Pallas kernels, body(): call(post_kernel, (2,), [SMEM, SMEM, SMEM, spec((8, 4, 2, 32, 128), lambd...  7.43 us
    pallas_call x1, Pallas kernels, body(): call(z_back, (3,), [spec((8, 1, 2, 32, N), lambda f: (0, f, 0, 0, 0)), wh...  6.13 us
    pallas_call x1, Pallas kernels, body(): call(pre_kernel, (8,), [SMEM, SMEM, SMEM, spec((3, 2, 1, 32, N), lambda i...  6.03 us
    pallas_call x1, Pallas kernels, body(): call(y_back, (3,), [spec((1, N, 2 * N), lambda f: (f, 0, 0)), spec((1, N,...  4.66 us
    pallas_call x1, Pallas kernels, body(): call(x_both, (2,), [spec((16, 3, 2, 8, N), lambda i: (0, 0, 0, 0, i)), wh...  4.37 us
  transfers between devices with their start and end apart: 1, of which 0 were waited for; matrix products, arithmetic and copies ran while one was open for 1% of the time, Pallas kernels for 0%

profile of v1, /device:TPU:1, one launch (start us, length us, event | category | flops | bytes accessed | tf_op | source)
XLA Modules:
  0.0 191.1 jit_solution(3579217254085010661)
XLA Ops:
  3.2 0.7 pad_add_fusion.place
  3.9 1.2 mul.14.offset
  5.1 0.6 pad_maximum_fusion.scal
  5.7 6.0 %shard_map.139 = (bf16[3,256,512]{2,1,0:T(8,128)(2,1)}, bf16[3,256,512]{2,1,0:T(8,128)(2,1)}, f32[8,8,128]{2,1,0:T(8,128)}) custom-call(s32[2]{0:T(128)} %pad_add_fusion.place, s32[8]{0:T(128)} %mul.14.offset, f32[4]{0:T(128)} %pad_maximum_fusion.scal, f32[3,2,8,32,256]{4,3,2,1,0:T(8,128)} %velocity.3), custom_call_target="tpu_custom_call" | custom-call | tf_op jit(solution)/shard_map/pallas_call | solution.py:275
  11.7 4.7 %shard_map.140 = f32[8,3,2,32,256]{4,3,2,1,0:T(8,128)} custom-call(bf16[3,256,512]{2,1,0:T(8,128)(2,1)} %get-tuple-element.8.high, bf16[3,256,512]{2,1,0:T(8,128)(2,1)} %get-tuple-element.9.low, bf16[2,512,512]{2,1,0:T(8,128)(2,1)} %constant.29.clone.first), custom_call_target="tpu_custom_call" | custom-call | tf_op jit(solution)/shard_map/pallas_call | solution.py:282
  16.4 26.5 %all_to_all.20.block = f32[8,3,2,32,256]{4,3,2,1,0:T(8,128)} all-to-all(f32[8,3,2,32,256]{4,3,2,1,0:T(8,128)} %shard_map.140), channel_id=1, replica_groups=mesh['row'=16,'col'=8] {'col'}, dimensions={0} | all-to-all | bytes 3145728 | tf_op jit(solution)/shard_map/all_to_all | solution.py:266
  42.9 6.1 %shard_map.141 = f32[16,3,2,8,512]{4,3,2,1,0:T(8,128)} custom-call(f32[8,3,2,32,256]{4,3,2,1,0:T(8,128)} %all_to_all.20.block, bf16[2,512,512]{2,1,0:T(8,128)(2,1)} %constant.30.clone.second), custom_call_target="tpu_custom_call" | custom-call | tf_op jit(solution)/shard_map/pallas_call | solution.py:288
  49.0 31.7 %all_to_all.21.block = f32[16,3,2,8,512]{4,3,2,1,0:T(8,128)} all-to-all(f32[16,3,2,8,512]{4,3,2,1,0:T(8,128)} %shard_map.141), channel_id=1, replica_groups=mesh['row'=16,'col'=8] {'row'}, dimensions={0} | all-to-all | bytes 3145728 | tf_op jit(solution)/shard_map/all_to_all | solution.py:266
  80.7 4.4 %shard_map.142 = f32[16,5,2,8,512]{4,3,2,1,0:T(8,128)} custom-call(f32[16,3,2,8,512]{4,3,2,1,0:T(8,128)} %all_to_all.21.block, bf16[2,256,176]{2,1,0:T(8,128)(2,1)} %constant.31.clone.back, bf16[2,176,256]{2,1,0:T(8,128)(2,1)} %constant.32.clone.fore), custom_call_target="tpu_custom_call" | custom-call | tf_op jit(solution)/shard_map/pallas_call | solution.py:295
  85.1 39.2 %all_to_all.22.block = f32[16,5,2,8,512]{4,3,2,1,0:T(8,128)} all-to-all(f32[16,5,2,8,512]{4,3,2,1,0:T(8,128)} %shard_map.142), channel_id=1, replica_groups=mesh['row'=16,'col'=8] {'row'}, dimensions={0} | all-to-all | bytes 5242880 | tf_op jit(solution)/shard_map/all_to_all | solution.py:266
  124.3 18.5 %shard_map.143 = f32[8,4,2,32,256]{4,3,2,1,0:T(8,128)} custom-call(s32[2]{0:T(128)} %pad_add_fusion.place, f32[16,5,2,8,512]{4,3,2,1,0:T(8,128)} %all_to_all.22.block, bf16[2,512,512]{2,1,0:T(8,128)(2,1)} %constant.29.clone.first), custom_call_target="tpu_custom_call" | custom-call | tf_op jit(solution)/shard_map/pallas_call | solution.py:301
  142.8 3.6 %all-to-all-start.3 = ((f32[8,4,2,32,256]{4,3,2,1,0:T(8,128)}), f32[8,4,2,32,256]{4,3,2,1,0:T(8,128)S(1)}, u32[]{:S(2)}, u32[]{:S(2)}) async-start(f32[8,4,2,32,256]{4,3,2,1,0:T(8,128)} %shard_map.143), calls=%async_computation.3 | async-start | bytes 4194304 | tf_op jit(solution)/shard_map/all_to_all | solution.py:266
  146.4 0.8 slice_reduce_fusion
  147.2 34.4 %psum.7 = f32[8,2]{1,0:T(8,128)S(1)} all-reduce(f32[8,2]{1,0:T(8,128)S(1)} %slice_reduce_fusion), channel_id=1, replica_groups=mesh['row'=16,'col'=8] {'col'}, use_global_device_ids=true, to_apply=%region_1.0 | all-reduce | flops 16 | bytes 128 | tf_op jit(solution)/shard_map/psum | solution.py:314
  181.6 0.1 maximum_multiply_fusion
  181.7 0.6 copy.15
  182.3 0.0 all-to-all-done.3.block
  182.3 0.0 copy-start
  182.3 1.4 copy-done
  183.7 7.4 %shard_map.144 = (f32[3,2,8,32,256]{4,3,2,1,0:T(8,128)}, f32[3,2,8,32,256]{4,3,2,1,0:T(8,128)}) custom-call(s32[2]{0:T(128)} %pad_add_fusion.place, s32[8]{0:T(128)} %mul.14.offset, f32[4]{0:T(128)} %pad_maximum_fusion.scal, f32[8,4,2,32,256]{4,3,2,1,0:T(8,128)} %copy-done, bf16[2,512,512]{2,1,0:T(8,128)(2,1)} %constant.30.clone.second, ...), custom_call_target="tpu_custom_call" | custom-call | tf_op jit(solution)/shard_map/pallas_call | solution.py:309
  (1 shorter events, 0.0 us)
Async XLA Ops:
  142.8 39.5 %all-to-all-start.3 = ((f32[8,4,2,32,256]{4,3,2,1,0:T(8,128)}), f32[8,4,2,32,256]{4,3,2,1,0:T(8,128)S(1)}, u32[]{:S(2)}, u32[]{:S(2)}) async-start(f32[8,4,2,32,256]{4,3,2,1,0:T(8,128)} %shard_map.143), calls=%async_computation.3 | async-start | bytes 4194304 | tf_op jit(solution)/shard_map/all_to_all | solution.py:266
  182.3 1.4 copy-start

commit v2 on v1

--- a/solution.py
+++ b/solution.py
@@ -112,90 +112,244 @@
     def total(value):
         value = jnp.sum(value, axis=0, keepdims=True)
         return value[:, :128] + value[:, 128:]
-    sums_out[0, 0:1, :] = total(stress)
-    sums_out[0, 1:2, :] = total(square * energy)
-
-
-def y_back(high, low, first, out):
-    result = dot3((first[0], first[1]), (high[0], low[0]), ((1,), (1,)))
-    for c in range(8):
-        for p in range(2):
-            out[c, 0, p] = result[p * N + 32 * c:p * N + 32 * c + 32]
-
-
-def z_back(block, second, out, data):
-    for p in range(2):
-        moved = swap_wide([block[s, 0, p] for s in range(8)])
-        for kx in range(8):
-            for g in range(2):
-                data[2 * p + g, pl.ds(kx, 32, stride=8), :] = moved[kx][:, 128 * g:128 * g + 128]
-    result = dot3(split(joined(data)), (second[0], second[1])).reshape(4, 8, 8, 2 * N)
-    for p in range(2):
+    sums_out[pl.ds(step, 1), :] = jnp.concatenate([total(stress), total(square * energy)], axis=1)
+
+
+MESH = pl.DeviceIdType.MESH
+
+
+def middle_kernel(high, low, sums, first, second, back, fore, hats_out, total_out,
+                  send_c, recv_c, send_r, recv_r, send_rf, recv_rf, send_cf, recv_cf, recv_s,
+                  u, hats, data, out_sems, in_sems):
+    row, col = lax.axis_index("row"), lax.axis_index("col")
+    row_on = row < ROWS
+    col_on = (col != 3) & (col != 4)
+    both_on = row_on & col_on
+
+    def push(src, dst, sem, **device):
+        return pltpu.make_async_remote_copy(
+            src_ref=src, dst_ref=dst, send_sem=out_sems.at[sem], recv_sem=in_sems.at[sem],
+            device_id=device, device_id_type=MESH)
+
+    def drain(ref, sem):
+        pltpu.make_async_copy(ref, ref, sem).wait()
+
+    barrier = pltpu.get_barrier_semaphore()
+    for i in range(1, 16):
+        pl.semaphore_signal(barrier, inc=1, device_id={"row": (row + i) % 16}, device_id_type=MESH)
+    for i in range(1, 8):
+        pl.semaphore_signal(barrier, inc=1, device_id={"col": (col + i) % 8}, device_id_type=MESH)
+    pl.semaphore_wait(barrier, 22)
+    for i in range(1, 8):
+        push(sums, recv_s.at[col], 15, col=(col + i) % 8).start()
+
+    @pl.when(both_on)
+    def _():
+        def y_back(f, carry):
+            result = dot3((first[0], first[1]), (high[f], low[f]), ((1,), (1,)))
+            for c in range(8):
+                for p in range(2):
+                    send_c[f, c, p] = result[p * N + 32 * c:p * N + 32 * c + 32]
+            for i in range(1, 8):
+                to = (col + i) % 8
+                push(send_c.at[f, to], recv_c.at[f, col], f, col=to).start()
+            recv_c[f, col] = send_c[f, col]
+            return carry
+
+        lax.fori_loop(0, 3, y_back, 0)
+
+    @pl.when(row_on)
+    def _():
+        def z_back(f, carry):
+            @pl.when(col_on)
+            def _():
+                drain(recv_c.at[f, pl.ds(0, 5)], in_sems.at[f])
+
+            @pl.when(jnp.logical_not(col_on))
+            def _():
+                drain(recv_c.at[f, pl.ds(0, 6)], in_sems.at[f])
+
+            for p in range(2):
+                blank = jnp.zeros((32, N), F32)
+                moved = swap_wide([blank if s in (3, 4) else recv_c[f, s, p] for s in range(8)])
+                for kx in range(8):
+                    for g in range(2):
+                        data[2 * p + g, pl.ds(kx, 32, stride=8), :] = moved[kx][:, 128 * g:128 * g + 128]
+            result = dot3(split(joined(data)), (second[0], second[1])).reshape(4, 8, 8, 2 * N)
+            for p in range(2):
+                for h in range(2):
+                    lanes = slice(p * N + 128 * h, p * N + 128 * h + 128)
+                    moved = swap_chunks([result[:, i, :, lanes] for i in range(8)], 16)
+                    for r in range(8):
+                        for j in range(4):
+                            send_r[f, 8 * h + r, p, :, 128 * j:128 * j + 128] = moved[r][j]
+            for i in range(1, 16):
+                to = (row + i) % 16
+                push(send_r.at[f, to], recv_r.at[f, row], 3 + f, row=to).start()
+            recv_r[f, row] = send_r[f, row]
+            return carry
+
+        lax.fori_loop(0, 3, z_back, 0)
+
+    count = ROWS * 8
+
+    def x_back(f, carry):
+        @pl.when(row_on)
+        def _():
+            drain(recv_r.at[f, pl.ds(0, ROWS - 1)], in_sems.at[3 + f])
+
+        @pl.when(jnp.logical_not(row_on))
+        def _():
+            drain(recv_r.at[f, pl.ds(0, ROWS)], in_sems.at[3 + f])
+
         for h in range(2):
-            lanes = slice(p * N + 128 * h, p * N + 128 * h + 128)
-            moved = swap_chunks([result[:, i, :, lanes] for i in range(8)], 16)
-            for r in range(8):
-                for j in range(4):
-                    out[8 * h + r, 0, p, :, 128 * j:128 * j + 128] = moved[r][j]
-
-
-def x_both(block, back, fore, out):
-    lanes = block.shape[-1]
-    count = ROWS * 8
-    u = []
-    for c in range(3):
-        both = jnp.concatenate([block[:ROWS, c, p].reshape(count, lanes) for p in range(2)], axis=0)
-        u.append(dot3((back[0], back[1]), split(both)))
-    square = u[0] * u[0]
-    fields = [u[0] * u[1], u[0] * u[2], u[1] * u[2], u[1] * u[1] - square, u[2] * u[2] - square]
-    for t in range(5):
-        hat = dot3((fore[0], fore[1]), split(fields[t])).reshape(2, ROWS, 8, lanes)
-        for p in range(2):
-            for r in range(ROWS):
-                out[r, t, p] = hat[p, r]
-            for r in range(ROWS, 16):
-                out[r, t, p] = jnp.zeros((8, lanes), F32)
-
-
-def z_fore(place, block, first, out, data, hats):
-    for t in range(5):
-        for p in range(2):
-            for h in range(2):
-                for j in range(4):
-                    moved = swap_chunks([block[8 * h + s, t, p, :, 128 * j:128 * j + 128] for s in range(8)], 16)
-                    for i in range(8):
-                        data[2 * p + h, (8 * j + i) * 8:(8 * j + i) * 8 + 8, :] = moved[i]
-        hats[t] = dot3(split(joined(data)), (first[0], first[1]))
-    kx_index = (lax.broadcasted_iota(jnp.int32, (N, N), 0) & 7) + place[0] * 8
-    kz_index = lax.broadcasted_iota(jnp.int32, (N, N), 1)
-    kx = kx_index.astype(F32)
-    kz = signed(kz_index).astype(F32)
-    origin = (kx_index == 0) & (kz_index == 0)
-    for p in range(2):
-        t01, t02, t12, t11, t22 = [hats[t, :, p * N:(p + 1) * N] for t in range(5)]
-        cross = kx * kz
-        fields = [
-            jnp.where(origin, t01, kx * t01 + kz * t12),
-            2.0 * cross * t02 + kz * kz * t22 - (kx * kx + kz * kz) * t11,
-            (kz * kz - kx * kx) * t02 - cross * t22,
-            jnp.where(origin, t12, kz * t01 - kx * t12),
-        ]
+            lanes = slice(N * h, N * h + N)
+            both = jnp.concatenate([recv_r[f, :ROWS, p, :, lanes].reshape(count, N) for p in range(2)], axis=0)
+            u[f, :, lanes] = dot3((back[0], back[1]), split(both))
+        return carry
+
+    lax.fori_loop(0, 3, x_back, 0)
+
+    def x_fore(t, carry):
+        a = jnp.where((t == 0) | (t == 2), 0, jnp.where(t == 3, 2, 1))
+        b = jnp.where((t == 0) | (t == 4), 1, 2)
+        weight = jnp.where(t >= 3, 1.0, 0.0)
+        for h in range(2):
+            lanes = slice(N * h, N * h + N)
+            field = u[a, :, lanes] * u[b, :, lanes] - weight * (u[0, :, lanes] * u[0, :, lanes])
+            hat = dot3((fore[0], fore[1]), split(field)).reshape(2, ROWS, 8, N)
+            for p in range(2):
+                for r in range(ROWS):
+                    send_rf[t, r, p, :, lanes] = hat[p, r]
+        for i in range(1, 16):
+            to = (row + i) % 16
+
+            @pl.when(to < ROWS)
+            def _():
+                push(send_rf.at[t, to], recv_rf.at[t, row], 6 + t, row=to).start()
+
+        @pl.when(row_on)
+        def _():
+            recv_rf[t, row] = send_rf[t, row]
+
+        return carry
+
+    lax.fori_loop(0, 5, x_fore, 0)
+
+    @pl.when(row_on)
+    def _():
+        def field_out(g, formula):
+            for p in range(2):
+                value = formula(p)
+                for h in range(2):
+                    data[h] = value[:, 128 * h:128 * h + 128]
+                moved = swap_wide([jnp.concatenate([data[h, pl.ds(i, 32, stride=8), :] for h in range(2)], axis=1)
+                                   for i in range(8)])
+                for c in range(8):
+                    if c not in (3, 4):
+                        send_cf[g, c, p] = moved[c]
+            for i in range(1, 8):
+                to = (col + i) % 8
+
+                @pl.when((to != 3) & (to != 4))
+                def _():
+                    push(send_cf.at[g, to], recv_cf.at[g, col], 11 + g, col=to).start()
+
+            @pl.when(col_on)
+            def _():
+                recv_cf[g, col] = send_cf[g, col]
+
+        def z_fore(t, carry):
+            drain(recv_rf.at[t, pl.ds(0, 15)], in_sems.at[6 + t])
+            for p in range(2):
+                for h in range(2):
+                    for j in range(4):
+                        moved = swap_chunks([recv_rf[t, 8 * h + s, p, :, 128 * j:128 * j + 128] for s in range(8)], 16)
+                        for i in range(8):
+                            data[2 * p + h, (8 * j + i) * 8:(8 * j + i) * 8 + 8, :] = moved[i]
+            hats[t] = dot3(split(joined(data)), (first[0], first[1]))
+
+            kx_index = (lax.broadcasted_iota(jnp.int32, (N, N), 0) & 7) + row * 8
+            kz_index = lax.broadcasted_iota(jnp.int32, (N, N), 1)
+            kx = kx_index.astype(F32)
+            kz = signed(kz_index).astype(F32)
+            origin = (kx_index == 0) & (kz_index == 0)
+
+            def part(number, p):
+                return hats[number, :, p * N:(p + 1) * N]
+
+            @pl.when(t == 1)
+            def _():
+                field_out(0, lambda p: jnp.where(origin, part(0, p), kx * part(0, p) + kz * part(1, p)))
+                field_out(3, lambda p: jnp.where(origin, part(1, p), kz * part(0, p) - kx * part(1, p)))
+
+            @pl.when(t == 3)
+            def _():
+                field_out(2, lambda p: (kz * kz - kx * kx) * part(2, p) - kx * kz * part(3, p))
+
+            @pl.when(t == 4)
+            def _():
+                field_out(1, lambda p: 2.0 * kx * kz * part(2, p) + kz * kz * part(3, p) - (kx * kx + kz * kz) * part(4, p))
+
+            return carry
+
+        lax.fori_loop(0, 5, z_fore, 0)
+
+    @pl.when(both_on)
+    def _():
+        def y_fore(step, carry):
+            g = jnp.where(step == 0, 0, 4 - step)
+            drain(recv_cf.at[g, pl.ds(0, 7)], in_sems.at[11 + g])
+            both = jnp.concatenate([recv_cf[g, :, p].reshape(N, N) for p in range(2)], axis=0)
+            hats_out[g] = dot3((second[0], second[1]), split(both))
+            return carry
+
+        lax.fori_loop(0, 4, y_fore, 0)
+
+    @pl.when(jnp.logical_not(both_on))
+    def _():
         for g in range(4):
-            for h in range(2):
-                data[h] = fields[g][:, 128 * h:128 * h + 128]
-            moved = swap_wide([jnp.concatenate([data[h, pl.ds(i, 32, stride=8), :] for h in range(2)], axis=1) for i in range(8)])
-            for c in range(8):
-                out[c, g, p] = moved[c]
-
-
-def post_kernel(place, offset, scal, block, second, velocity, accumulator, new_velocity, new_accumulator):
+            hats_out[g] = jnp.zeros((2 * N, N), F32)
+
+    drain(recv_s.at[pl.ds(0, 7)], in_sems.at[15])
+    recv_s[col] = sums[...]
+    total = recv_s[0]
+    for i in range(1, 8):
+        total = total + recv_s[i]
+    total_out[...] = total
+
+    drain(recv_s.at[pl.ds(0, 7)], out_sems.at[15])
+
+    @pl.when(both_on)
+    def _():
+        for f in range(3):
+            drain(send_c.at[f, pl.ds(0, 7)], out_sems.at[f])
+
+    @pl.when(row_on)
+    def _():
+        for f in range(3):
+            drain(send_r.at[f, pl.ds(0, 15)], out_sems.at[3 + f])
+        for t in range(5):
+            drain(send_rf.at[t, pl.ds(0, ROWS - 1)], out_sems.at[6 + t])
+        for g in range(4):
+            @pl.when(col_on)
+            def _():
+                drain(send_cf.at[g, pl.ds(0, 5)], out_sems.at[11 + g])
+
+            @pl.when(jnp.logical_not(col_on))
+            def _():
+                drain(send_cf.at[g, pl.ds(0, 6)], out_sems.at[11 + g])
+
+    @pl.when(jnp.logical_not(row_on))
+    def _():
+        for t in range(5):
+            drain(send_rf.at[t, pl.ds(0, ROWS)], out_sems.at[6 + t])
+
+
+def post_kernel(place, offset, scal, block, velocity, accumulator, new_velocity, new_accumulator):
     step = pl.program_id(0)
     drift = scal[1] * scal[2]
-    hats = []
-    for g in range(4):
-        both = jnp.concatenate([block[:, g, p].reshape(N, 128) for p in range(2)], axis=0)
-        result = dot3((second[0], second[1]), split(both))
-        hats.append((result[:N], result[N:]))
+    hats = [(block[g, :N], block[g, N:]) for g in range(4)]
     lane = lax.broadcasted_iota(jnp.int32, (N, 128), 1)
     kx_index = lane // 32 + (place[0] * 8 + step * 4)
     kz_index = lane % 32 + place[1] * 32
@@ -262,10 +416,6 @@
 SMEM = pl.BlockSpec(memory_space=pltpu.SMEM)
 
 
-def exchange(value, axis):
-    return lax.all_to_all(value, axis, split_axis=0, concat_axis=0, tiled=True)
-
-
 def body(velocity, accumulator, remesh_flag, remesh_shift, viscosity, shear, clock, step):
     first, second, back, fore = [jnp.asarray(table) for table in tables()]
     place = jnp.stack([lax.axis_index("row"), lax.axis_index("col")]).astype(jnp.int32)
@@ -277,41 +427,32 @@
         [SMEM, SMEM, SMEM, spec((3, 2, 1, 32, N), lambda i: (0, 0, i, 0, 0))],
         [(spec((3, 32, 2 * N), lambda i: (0, i, 0)), shape((3, N, 2 * N), BF16)),
          (spec((3, 32, 2 * N), lambda i: (0, i, 0)), shape((3, N, 2 * N), BF16)),
-         (spec((1, 8, 128), lambda i: (i, 0, 0)), shape((8, 8, 128), F32))],
+         (spec((8, N), lambda i: (0, 0)), shape((8, N), F32))],
     )(place, offset, scal, velocity)
-    [one] = call(
-        y_back, (3,),
-        [spec((1, N, 2 * N), lambda f: (f, 0, 0)), spec((1, N, 2 * N), lambda f: (f, 0, 0)), whole(first)],
-        [(spec((8, 1, 2, 32, N), lambda f: (0, f, 0, 0, 0)), shape((8, 3, 2, 32, N), F32))],
-    )(high, low, first)
-    one = exchange(one, "col")
-    [two] = call(
-        z_back, (3,),
-        [spec((8, 1, 2, 32, N), lambda f: (0, f, 0, 0, 0)), whole(second)],
-        [(spec((16, 1, 2, 8, 2 * N), lambda f: (0, f, 0, 0, 0)), shape((16, 3, 2, 8, 2 * N), F32))],
-        [pltpu.VMEM((4, N, 128), F32)],
-    )(one, second)
-    two = exchange(two, "row")
-    [three] = call(
-        x_both, (2,),
-        [spec((16, 3, 2, 8, N), lambda i: (0, 0, 0, 0, i)), whole(back), whole(fore)],
-        [(spec((16, 5, 2, 8, N), lambda i: (0, 0, 0, 0, i)), shape((16, 5, 2, 8, 2 * N), F32))],
-    )(two, back, fore)
-    three = exchange(three, "row")
-    [four] = call(
-        z_fore, (1,),
-        [SMEM, whole(three), whole(first)],
-        [(spec((8, 4, 2, 32, N), lambda i: (0, 0, 0, 0, 0)), shape((8, 4, 2, 32, N), F32))],
-        [pltpu.VMEM((4, N, 128), F32), pltpu.VMEM((5, N, 2 * N), F32)],
-    )(place, three, first)
-    four = exchange(four, "col")
+    vmem = pl.BlockSpec(memory_space=pltpu.VMEM)
+    hats, total = pl.pallas_call(
+        middle_kernel,
+        in_specs=[vmem] * 7,
+        out_specs=[vmem] * 2,
+        out_shape=[shape((4, 2 * N, N), F32), shape((8, N), F32)],
+        scratch_shapes=[
+            pltpu.VMEM((3, 8, 2, 32, N), F32), pltpu.VMEM((3, 8, 2, 32, N), F32),
+            pltpu.VMEM((3, 16, 2, 8, 2 * N), F32), pltpu.VMEM((3, 16, 2, 8, 2 * N), F32),
+            pltpu.VMEM((5, 16, 2, 8, 2 * N), F32), pltpu.VMEM((5, 16, 2, 8, 2 * N), F32),
+            pltpu.VMEM((4, 8, 2, 32, N), F32), pltpu.VMEM((4, 8, 2, 32, N), F32),
+            pltpu.VMEM((8, 8, N), F32),
+            pltpu.VMEM((3, N, 2 * N), F32), pltpu.VMEM((5, N, 2 * N), F32), pltpu.VMEM((4, N, 128), F32),
+            pltpu.SemaphoreType.DMA((16,)), pltpu.SemaphoreType.DMA((16,)),
+        ],
+        compiler_params=pltpu.CompilerParams(collective_id=0, has_side_effects=True, vmem_limit_bytes=VLIM),
+    )(high, low, sums, first, second, back, fore)
     state = spec((3, 2, 4, 32, N), lambda i: (0, 0, i, 0, 0))
     new_velocity, new_accumulator = call(
         post_kernel, (2,),
-        [SMEM, SMEM, SMEM, spec((8, 4, 2, 32, 128), lambda i: (0, 0, 0, 0, i)), whole(second), state, state],
+        [SMEM, SMEM, SMEM, spec((4, 2 * N, 128), lambda i: (0, 0, i)), state, state],
         [(state, shape(velocity.shape, F32)), (state, shape(velocity.shape, F32))],
-    )(place, offset, scal, four, second, velocity, accumulator)
-    total = lax.psum(jnp.sum(sums[:, :2], axis=2), "col")
+    )(place, offset, scal, hats, velocity, accumulator)
+    total = jnp.sum(total.reshape(8, 2, 128), axis=2)
     scale = jnp.stack([jnp.ones((), F32), 2.0 * viscosity[0]]) / (N * N)
     return new_velocity, new_accumulator, total.T * scale[:, None]
 

time: 195 us -> 124 us (0.64); the launches traced: 191 us -> 123 us
  blocking collectives: 132 us -> 0 us
  Pallas kernels: 47.1 us -> 116 us
  starting transfers between devices: 3.6 us -> 0 us
  local copies, waits for them, and re-layouts: 1.99 us -> 0 us
    all_to_all x3 -> x0, blocking collectives: 97.5 us -> none  [exchange(): return lax.all_to_all(value, axis, split_axis=0, concat_axis=0, tiled=True)]
    pallas_call x5 -> x2, Pallas kernels: 41 us -> 110 us  [the longest x1 106 us: body(): pl.pallas_call(middle_kernel, in_specs=[vmem] * 7, out_specs=[vmem] * 2,...]
    psum x1 -> x0, blocking collectives: 34.4 us -> none  [body(): total = lax.psum(jnp.sum(sums[:, :2], axis=2), 'col')]
    all_to_all x1 -> x0, starting transfers between devices: 3.6 us -> none  [exchange(): return lax.all_to_all(value, axis, split_axis=0, concat_axis=0, tiled=True)]
    unnamed x3 -> x0, local copies, waits for them, and re-layouts: 1.99 us -> none
  transfers between devices with their start and end apart: 1 -> 0, of which waited for: 0 -> 0; matrix products, arithmetic and copies ran while one was open for 1% -> 0% of each run, Pallas kernels for 0% -> 0%
where the time goes in v2:
time: 124 us; the launch traced here: 123 us
  Pallas kernels  116 us (94%)
  other arithmetic  3.88 us (3%)
  between operations  3.23 us (3%)
    pallas_call x1, Pallas kernels, body(): pl.pallas_call(middle_kernel, in_specs=[vmem] * 7, out_specs=[vmem] * 2,...  106 us
    pallas_call x1, Pallas kernels, body(): call(pre_kernel, (8,), [SMEM, SMEM, SMEM, spec((3, 2, 1, 32, N), lambda i...  6.05 us
    pallas_call x1, Pallas kernels, body(): call(post_kernel, (2,), [SMEM, SMEM, SMEM, spec((4, 2 * N, 128), lambda i...  4.67 us

profile of v2, /device:TPU:1, one launch (start us, length us, event | category | flops | bytes accessed | tf_op | source)
XLA Modules:
  0.0 123.5 jit_solution(14436668990018722339)
XLA Ops:
  3.2 0.6 pad_maximum_fusion.scal
  3.8 0.6 pad_add_fusion.place
  4.4 0.1 maximum_multiply_fusion
  4.4 1.2 %mul.14.offset = s32[8]{0:T(128)} multiply(s32[8]{0:T(128)} %param.14, s32[8]{0:T(128)} %param.15) | non-fusion elementwise | flops 8 | bytes 96 | tf_op jit(solution)/shard_map/mul | solution.py:422
  5.7 6.0 %shard_map.139 = (bf16[3,256,512]{2,1,0:T(8,128)(2,1)}, bf16[3,256,512]{2,1,0:T(8,128)(2,1)}, f32[8,256]{1,0:T(8,128)}) custom-call(s32[2]{0:T(128)} %pad_add_fusion.place, s32[8]{0:T(128)} %mul.14.offset, f32[4]{0:T(128)} %pad_maximum_fusion.scal, f32[3,2,8,32,256]{4,3,2,1,0:T(8,128)} %velocity.3), custom_call_target="tpu_custom_call" | custom-call | tf_op jit(solution)/shard_map/pallas_call | solution.py:425
  11.7 105.6 %shard_map.140 = (f32[4,512,256]{2,1,0:T(8,128)}, f32[8,256]{1,0:T(8,128)}) custom-call(bf16[3,256,512]{2,1,0:T(8,128)(2,1)} %get-tuple-element.10.high, bf16[3,256,512]{2,1,0:T(8,128)(2,1)} %get-tuple-element.11.low, f32[8,256]{1,0:T(8,128)} %get-tuple-element.12.sums, bf16[2,512,512]{2,1,0:T(8,128)(2,1)} %constant.29.clone.first, ...), custom_call_target="tpu_custom_call" | custom-call | tf_op jit(solution)/shard_map/pallas_call | solution.py:433
  117.4 0.8 bitcast_reduce_fusion
  118.2 0.6 multiply_bitcast_fusion
  118.8 4.7 %shard_map.141 = (f32[3,2,8,32,256]{4,3,2,1,0:T(8,128)}, f32[3,2,8,32,256]{4,3,2,1,0:T(8,128)}) custom-call(s32[2]{0:T(128)} %pad_add_fusion.place, s32[8]{0:T(128)} %mul.14.offset, f32[4]{0:T(128)} %pad_maximum_fusion.scal, f32[4,512,256]{2,1,0:T(8,128)} %get-tuple-element.13.block, f32[3,2,8,32,256]{4,3,2,1,0:T(8,128)} %velocity.3, ...), custom_call_target="tpu_custom_call" | custom-call | tf_op jit(solution)/shard_map/pallas_call | solution.py:450

commit v3 on v1

v3 whole, which is shorter than its diff:
```python
import numpy as np
import jax
import jax.numpy as jnp
from jax import lax
from jax.experimental import pallas as pl
from jax.experimental.pallas import tpu as pltpu
from jax.sharding import PartitionSpec as P

N = 256
ROWS = 11
COLS = (0, 1, 2, 5, 6, 7)
KX = 8 * ROWS
F32 = jnp.float32
BF16 = jnp.bfloat16
VLIM = 60 * 1024 * 1024


def halves(table):
    table = table.astype(np.float32)
    high = table.astype(jnp.bfloat16)
    low = (table - high.astype(np.float32)).astype(jnp.bfloat16)
    return np.stack([high, low])


def tables():
    index = np.arange(N)
    angle = (index[:, None] * index[None, :] % N) * (2.0 * np.pi / N)
    cos, sin = np.cos(angle) / 16.0, np.sin(angle) / 16.0
    first = np.block([[cos, -sin], [sin, cos]])
    second = np.block([[cos, sin], [-sin, cos]])
    place = np.arange(KX)
    order = 4 * (place % 22) + place // 22
    weights = np.where(order == 0, 1.0, 2.0)
    back_x = np.concatenate([cos[:, order] * weights, -sin[:, order] * weights], axis=1)
    fore_x = np.concatenate([cos[order], -sin[order]], axis=0)
    return halves(first), halves(second), halves(back_x), halves(fore_x)


def split(value):
    high = value.astype(BF16)
    return high, (value - high.astype(F32)).astype(BF16)


def dot3(left, right, dims=((1,), (0,))):
    def one(a, b):
        return lax.dot_general(a, b, (dims, ((), ())), preferred_element_type=F32)

    return one(left[0], right[0]) + one(left[1], right[0]) + one(left[0], right[1])


def swap_chunks(items, width):
    items = list(items)
    count = len(items)
    lane = lax.broadcasted_iota(jnp.int32, items[0].shape, items[0].ndim - 1) // width
    axis = items[0].ndim - 1
    step = count // 2
    while step:
        keep = (lane & step) == 0
        for i in range(count):
            if i & step == 0:
                a, b = items[i], items[i + step]
                items[i] = jnp.where(keep, a, pltpu.roll(b, step * width, axis))
                items[i + step] = jnp.where(keep, pltpu.roll(a, 128 - step * width, axis), b)
        step //= 2
    return items


def signed(index):
    return jnp.where(2 * index < N, index, index - N)


def modes(kx_index, kz_index, ky_index, drift):
    wave_x = kx_index.astype(F32)
    wave_z = signed(kz_index).astype(F32)
    wave_y = signed(ky_index).astype(F32) - drift * wave_x
    square = wave_x * wave_x + wave_y * wave_y + wave_z * wave_z
    mask = (3 * kx_index < N) & (3 * jnp.abs(signed(kz_index)) < N) & (3 * jnp.abs(signed(ky_index)) < N)
    return wave_x, wave_y, wave_z, square, mask


def pre_kernel(flag, amount, shear, clock, velocity, high_out, low_out, sums_out):
    step = pl.program_id(0)
    shift = (0 - flag[step] * amount[step]) & (N - 1)
    kx = jnp.full((32, N), lax.axis_index("row") * 8 + step, jnp.int32)
    kz = lax.broadcasted_iota(jnp.int32, (32, N), 0) + lax.axis_index("col") * 32
    ky = lax.broadcasted_iota(jnp.int32, (32, N), 1)
    wave_x, wave_y, wave_z, square, mask = modes(kx, kz, ky, shear[0] * clock[0])
    inverse = 1.0 / jnp.maximum(square, 1.0)
    wave = (wave_x, wave_y, wave_z)
    energy = jnp.zeros((32, N), F32)
    stress = jnp.zeros((32, N), F32)
    for p in range(2):
        v = [pltpu.roll(velocity[c, p, 0], shift, 1) for c in range(3)]
        energy += v[0] * v[0] + v[1] * v[1] + v[2] * v[2]
        stress += v[0] * v[1]
        along = (wave[0] * v[0] + wave[1] * v[1] + wave[2] * v[2]) * inverse
        for c in range(3):
            high, low = split(jnp.where(mask, v[c] - wave[c] * along, 0.0))
            high_out[c, :, p * N:(p + 1) * N] = high
            low_out[c, :, p * N:(p + 1) * N] = low
    def total(value):
        value = jnp.sum(value, axis=0, keepdims=True)
        return value[:, :128] + value[:, 128:]
    sums_out[pl.ds(step, 1), :] = jnp.concatenate([total(stress), total(square * energy)], axis=1)


MESH = pl.DeviceIdType.MESH


def middle_kernel(high, low, sums, first, second, back, fore, hats_out, total_out,
                  send_b, recv_b, send_f, recv_f, recv_s, u, hats, data, out_sems, in_sems):
    row, col = lax.axis_index("row"), lax.axis_index("col")
    me = row * 8 + col
    on = (row < ROWS) & (col != 3) & (col != 4)
    off = jnp.logical_not(on)

    def push(src, dst, sem, device):
        return pltpu.make_async_remote_copy(
            src_ref=src, dst_ref=dst, send_sem=out_sems.at[sem], recv_sem=in_sems.at[sem],
            device_id=device, device_id_type=MESH)

    def drain(blocks, sem):
        ref = recv_f.at[0, pl.ds(0, 8 * blocks)]
        pltpu.make_async_copy(ref, ref, sem).wait()

    barrier = pltpu.get_barrier_semaphore()

    def greet(i, carry):
        to = lax.rem(me + i, 128)
        pl.semaphore_signal(barrier, inc=1, device_id={"row": to // 8, "col": lax.rem(to, 8)}, device_id_type=MESH)
        return carry

    lax.fori_loop(1, 128, greet, 0)
    pl.semaphore_wait(barrier, 127)
    for i in range(1, 8):
        push(sums, recv_s.at[col], 7, {"col": (col + i) % 8}).start()

    @pl.when(on)
    def _():
        def y_back(f, carry):
            result = dot3((first[0], first[1]), (high[f], low[f]), ((1,), (1,)))
            for h in range(2):
                for plane in range(2):
                    for p in range(2):
                        start = p * N + plane * 128
                        send_b[f, pl.ds((h * 2 + plane) * 2 + p, 128, stride=8), :] = (
                            result[start:start + 128, 128 * h:128 * h + 128])

            def send(i, carry):
                to = lax.rem(me + i, 128)
                push(send_b.at[f, pl.ds(to * 8, 8)], recv_b.at[f, col, pl.ds(row * 8, 8)], f,
                     {"row": to // 8, "col": lax.rem(to, 8)}).start()
                return carry

            lax.fori_loop(1, 128, send, 0)
            recv_b[f, col, pl.ds(row * 8, 8), :] = send_b[f, pl.ds(me * 8, 8), :]
            return carry

        lax.fori_loop(0, 3, y_back, 0)

    def to_grid(f):
        @pl.when(on)
        def _():
            drain(65, in_sems.at[f])

        @pl.when(off)
        def _():
            drain(66, in_sems.at[f])

        for g in range(2):
            blocks = [recv_b[f, c] if c in COLS else jnp.zeros((KX, 128), F32) for c in range(4 * g, 4 * g + 4)]
            moved = swap_chunks(blocks, 32)
            for i in range(4):
                data[g, KX * i:KX * i + KX, :] = moved[i]
        modes_in = jnp.concatenate(
            [jnp.concatenate([data[g, pl.ds(plane * 2 + p, KX, stride=4), :] for p in range(2) for g in range(2)], axis=1)
             for plane in range(2)], axis=0)
        lines = dot3(split(modes_in), (second[0], second[1]))
        for plane in range(2):
            both = jnp.concatenate([lines[KX * plane:KX * plane + KX, p * N:p * N + N] for p in range(2)], axis=0)
            u[f, :, plane * N:plane * N + N] = dot3((back[0], back[1]), split(both))

    def to_modes(t):
        a = jnp.where((t == 0) | (t == 3), 0, jnp.where(t == 4, 2, 1))
        b = jnp.where(t < 2, 1, 2)
        weight = jnp.where((t == 1) | (t == 4), 1.0, 0.0)
        planes = []
        for plane in range(2):
            lanes = slice(plane * N, plane * N + N)
            field = u[a, :, lanes] * u[b, :, lanes] - weight * (u[0, :, lanes] * u[0, :, lanes])
            hat = dot3((fore[0], fore[1]), split(field))
            planes.append(jnp.concatenate([hat[:KX], hat[KX:]], axis=1))
        hats[t] = dot3(split(jnp.concatenate(planes, axis=0)), (first[0], first[1]))

    place = lax.broadcasted_iota(jnp.int32, (KX, N), 0)
    group = (place >= 22).astype(jnp.int32) + (place >= 44).astype(jnp.int32) + (place >= 66).astype(jnp.int32)
    kx_index = 4 * (place - 22 * group) + group
    kz_index = lax.broadcasted_iota(jnp.int32, (KX, N), 1)
    kx = kx_index.astype(F32)
    kz = signed(kz_index).astype(F32)
    origin = (kx_index == 0) & (kz_index == 0)

    def field_out(g, formula):
        for plane in range(2):
            for p in range(2):
                value = formula(lambda t: hats[t, plane * KX:plane * KX + KX, p * N:p * N + N])
                for half in range(2):
                    data[half, pl.ds(plane * 2 + p, KX, stride=4), :] = value[:, 128 * half:128 * half + 128]
        for half in range(2):
            moved = swap_chunks([data[half, KX * i:KX * i + KX, :] for i in range(4)], 32)
            for i in range(4):
                if 4 * half + i in COLS:
                    send_f[g, 4 * half + i] = moved[i]

        def send(i, carry):
            number = lax.rem(me + i, 6 * ROWS)
            to_row, spot = number // 6, lax.rem(number, 6)
            to_col = spot + 2 * (spot // 3)

            @pl.when((to_row != row) | (to_col != col))
            def _():
                push(send_f.at[g, to_col, pl.ds(to_row * 8, 8)], recv_f.at[g, pl.ds(me * 8, 8)], 3 + g,
                     {"row": to_row, "col": to_col}).start()

            return carry

        lax.fori_loop(0, 6 * ROWS, send, 0)

        @pl.when(on)
        def _():
            recv_f[g, pl.ds(me * 8, 8), :] = send_f[g, col, pl.ds(row * 8, 8), :]

    def step_of(step, carry):
        backward = (step == 0) | (step == 1) | (step == 4)

        @pl.when(backward)
        def _():
            to_grid(jnp.where(step == 4, 2, jnp.minimum(step, 2)))

        @pl.when(jnp.logical_not(backward))
        def _():
            to_modes(jnp.where(step < 4, step - 2, step - 3))

        @pl.when(step == 5)
        def _():
            field_out(0, lambda t: jnp.where(origin, t(0), kx * t(0) + kz * t(2)))
            field_out(1, lambda t: jnp.where(origin, t(2), kz * t(0) - kx * t(2)))

        @pl.when(step == 7)
        def _():
            field_out(2, lambda t: (kz * kz - kx * kx) * t(3) - kx * kz * t(4))
            field_out(3, lambda t: 2.0 * kx * kz * t(3) + kz * kz * t(4) - (kx * kx + kz * kz) * t(1))

        return carry

    lax.fori_loop(0, 8, step_of, 0)

    drain_sums = recv_s.at[pl.ds(0, 7)]
    pltpu.make_async_copy(drain_sums, drain_sums, in_sems.at[7]).wait()
    recv_s[col] = sums[...]
    total = recv_s[0]
    for i in range(1, 8):
        total = total + recv_s[i]
    total_out[...] = total

    @pl.when(on)
    def _():
        def y_fore(g, carry):
            drain(127, in_sems.at[3 + g])
            both = jnp.concatenate(
                [jnp.concatenate([recv_f[g, pl.ds((h * 2 + plane) * 2 + p, 128, stride=8), :] for h in range(2)], axis=1)
                 for p in range(2) for plane in range(2)], axis=0)
            hats_out[g] = dot3((second[0], second[1]), split(both))
            return carry

        lax.fori_loop(0, 4, y_fore, 0)

    @pl.when(off)
    def _():
        for g in range(4):
            hats_out[g] = jnp.zeros((2 * N, N), F32)

    pltpu.make_async_copy(drain_sums, drain_sums, out_sems.at[7]).wait()

    @pl.when(on)
    def _():
        for f in range(3):
            drain(127, out_sems.at[f])
        for g in range(4):
            drain(65, out_sems.at[3 + g])

    @pl.when(off)
    def _():
        for g in range(4):
            drain(66, out_sems.at[3 + g])


def post_kernel(flag, amount, viscosity, shear, clock, time_step, total, block, velocity, accumulator,
                new_velocity, new_accumulator, spectra):
    step = pl.program_id(0)
    row, col = lax.axis_index("row"), lax.axis_index("col")
    drift = shear[0] * clock[0]

    @pl.when(step == 0)
    def _():
        diagonal = lax.broadcasted_iota(jnp.int32, (8, 8), 0) == lax.broadcasted_iota(jnp.int32, (8, 8), 1)
        for i, factor in enumerate((1.0, 2.0 * viscosity[0])):
            value = jnp.sum(total[:, 128 * i:128 * i + 128], axis=1, keepdims=True) * (factor / (N * N))
            spectra[i:i + 1, :] = jnp.sum(jnp.where(diagonal, value, 0.0), axis=0, keepdims=True)

    hats = [(block[g, :N], block[g, N:]) for g in (0, 3, 2, 1)]
    lane = lax.broadcasted_iota(jnp.int32, (N, 128), 1)
    kx_index = lane // 32 + (row * 8 + step * 4)
    kz_index = lane % 32 + col * 32
    ky_index = lax.broadcasted_iota(jnp.int32, (N, 128), 0)
    kx, k1, kz, square, mask = modes(kx_index, kz_index, ky_index, drift)
    flat = kx * kx + kz * kz
    origin = flat == 0.0
    over_square = 1.0 / jnp.maximum(square, 1.0)
    over_flat = 1.0 / jnp.maximum(flat, 1.0)
    result = [[None, None] for _ in range(3)]
    for p in range(2):
        sign = -1.0 if p == 0 else 1.0
        x, q, r, s = [sign * hats[g][1 - p] for g in range(4)]
        v = ((k1 * k1 - flat) * x + k1 * q) * over_square
        w = 0.0 - (r + k1 * s)
        part = [
            jnp.where(origin, 0.0 - k1 * x, (kz * w - kx * k1 * v) * over_flat),
            jnp.where(origin, 0.0, v),
            jnp.where(origin, 0.0 - k1 * s, (0.0 - kx * w - kz * k1 * v) * over_flat),
        ]
        for c in range(3):
            result[c][p] = jnp.where(mask, part[c], 0.0).T
    for i in range(4):
        shift = (0 - flag[step * 4 + i] * amount[step * 4 + i]) & (N - 1)
        kx_index = jnp.full((32, N), row * 8 + step * 4 + i, jnp.int32)
        kz_index = lax.broadcasted_iota(jnp.int32, (32, N), 0) + col * 32
        ky_index = lax.broadcasted_iota(jnp.int32, (32, N), 1)
        kx, k1, kz, square, _ = modes(kx_index, kz_index, ky_index, drift)
        wave = (kx, k1, kz)
        coupling = 2.0 * shear[0] * kx / jnp.maximum(square, 1.0)
        damp = viscosity[0] * square
        for p in range(2):
            v = [pltpu.roll(velocity[c, p, i], shift, 1) for c in range(3)]
            for c in range(3):
                rate = result[c][p][32 * i:32 * i + 32] + coupling * wave[c] * v[1] - damp * v[c]
                if c == 0:
                    rate = rate - shear[0] * v[1]
                fresh = (-5.0 / 9.0) * pltpu.roll(accumulator[c, p, i], shift, 1) + time_step[0] * rate
                new_accumulator[c, p, i] = fresh
                new_velocity[c, p, i] = v[c] + (15.0 / 16.0) * fresh


def call(kernel, grid, ins, outs, scratch=()):
    return pl.pallas_call(
        kernel,
        grid=grid,
        in_specs=ins,
        out_specs=[spec for spec, _ in outs],
        out_shape=[shape for _, shape in outs],
        scratch_shapes=list(scratch),
        compiler_params=pltpu.CompilerParams(vmem_limit_bytes=VLIM),
    )


def spec(shape, index):
    return pl.BlockSpec(shape, index)


def whole(array):
    rank = array.ndim
    return pl.BlockSpec(array.shape, lambda *_: (0,) * rank)


SMEM = pl.BlockSpec(memory_space=pltpu.SMEM)


def body(velocity, accumulator, remesh_flag, remesh_shift, viscosity, shear, clock, step):
    first, second, back, fore = [jnp.asarray(table) for table in tables()]
    shape = jax.ShapeDtypeStruct
    high, low, sums = call(
        pre_kernel, (8,),
        [SMEM] * 4 + [spec((3, 2, 1, 32, N), lambda i: (0, 0, i, 0, 0))],
        [(spec((3, 32, 2 * N), lambda i: (0, i, 0)), shape((3, N, 2 * N), BF16)),
         (spec((3, 32, 2 * N), lambda i: (0, i, 0)), shape((3, N, 2 * N), BF16)),
         (spec((8, N), lambda i: (0, 0)), shape((8, N), F32))],
    )(remesh_flag, remesh_shift, shear, clock, velocity)
    vmem = pl.BlockSpec(memory_space=pltpu.VMEM)
    hats, total = pl.pallas_call(
        middle_kernel,
        in_specs=[vmem] * 7,
        out_specs=[vmem] * 2,
        out_shape=[shape((4, 2 * N, N), F32), shape((8, N), F32)],
        scratch_shapes=[
            pltpu.VMEM((3, 1024, 128), F32), pltpu.VMEM((3, 8, KX, 128), F32),
            pltpu.VMEM((4, 8, KX, 128), F32), pltpu.VMEM((4, 1024, 128), F32),
            pltpu.VMEM((8, 8, N), F32),
            pltpu.VMEM((3, N, 2 * N), F32), pltpu.VMEM((5, 2 * KX, 2 * N), F32), pltpu.VMEM((2, 4 * KX, 128), F32),
            pltpu.SemaphoreType.DMA((8,)), pltpu.SemaphoreType.DMA((8,)),
        ],
        compiler_params=pltpu.CompilerParams(collective_id=0, has_side_effects=True, vmem_limit_bytes=VLIM),
    )(high, low, sums, first, second, back, fore)
    state = spec((3, 2, 4, 32, N), lambda i: (0, 0, i, 0, 0))
    return call(
        post_kernel, (2,),
        [SMEM] * 6 + [spec((8, N), lambda i: (0, 0)), spec((4, 2 * N, 128), lambda i: (0, 0, i)), state, state],
        [(state, shape(velocity.shape, F32)), (state, shape(velocity.shape, F32)),
         (spec((2, 8), lambda i: (0, 0)), shape((2, 8), F32))],
    )(remesh_flag, remesh_shift, viscosity, shear, clock, step, total, hats, velocity, accumulator)


def solution(mesh):
    state = P(None, None, "row", "col", None)
    return jax.shard_map(
        body,
        mesh=mesh,
        in_specs=(state, state, P("row"), P("row"), P(), P(), P(), P()),
        out_specs=(state, state, P(None, "row")),
        check_vma=False,
    )
```

time: 195 us -> 79.2 us (0.41); the launches traced: 191 us -> 78.9 us
  blocking collectives: 132 us -> 0 us
  Pallas kernels: 47.1 us -> 75.7 us
  starting transfers between devices: 3.6 us -> 0 us
  other arithmetic: 3.38 us -> 0 us
  local copies, waits for them, and re-layouts: 1.99 us -> 0 us
    all_to_all x3 -> x0, blocking collectives: 97.5 us -> none  [exchange(): return lax.all_to_all(value, axis, split_axis=0, concat_axis=0, tiled=True)]
    psum x1 -> x0, blocking collectives: 34.4 us -> none  [body(): total = lax.psum(jnp.sum(sums[:, :2], axis=2), 'col')]
    pallas_call x6 -> x3, Pallas kernels: 47.1 us -> 75.7 us  [the longest x1 64.8 us: body(): pl.pallas_call(middle_kernel, in_specs=[vmem] * 7, out_specs=[vmem] * 2,...]
    all_to_all x1 -> x0, starting transfers between devices: 3.6 us -> none  [exchange(): return lax.all_to_all(value, axis, split_axis=0, concat_axis=0, tiled=True)]
    unnamed x3 -> x0, local copies, waits for them, and re-layouts: 1.99 us -> none
  transfers between devices with their start and end apart: 1 -> 0, of which waited for: 0 -> 0; matrix products, arithmetic and copies ran while one was open for 1% -> 0% of each run, Pallas kernels for 0% -> 0%
where the time goes in v3:
time: 79.2 us; the launch traced here: 78.9 us
  Pallas kernels  75.7 us (96%)
  between operations  3.22 us (4%)
    pallas_call x1, Pallas kernels, body(): pl.pallas_call(middle_kernel, in_specs=[vmem] * 7, out_specs=[vmem] * 2,...  64.8 us
    pallas_call x1, Pallas kernels, body(): call(pre_kernel, (8,), [SMEM] * 4 + [spec((3, 2, 1, 32, N), lambda i: (0,...  6.08 us
    pallas_call x1, Pallas kernels, body(): call(post_kernel, (2,), [SMEM] * 6 + [spec((8, N), lambda i: (0, 0)), spe...  4.8 us

profile of v3, /device:TPU:1, one launch (start us, length us, event | category | flops | bytes accessed | tf_op | source)
XLA Modules:
  0.0 78.9 jit_solution(17822961649784824482)
XLA Ops:
  3.2 6.1 %shard_map.139 = (bf16[3,256,512]{2,1,0:T(8,128)(2,1)}, bf16[3,256,512]{2,1,0:T(8,128)(2,1)}, f32[8,256]{1,0:T(8,128)}) custom-call(s32[8]{0:T(128)} %flag.3, s32[8]{0:T(128)} %amount.3, f32[1]{0:T(128)S(6)} %copy.16.shear, f32[1]{0:T(128)S(6)} %copy.17.clock, f32[3,2,8,32,256]{4,3,2,1,0:T(8,128)} %velocity.3), custom_call_target="tpu_custom_call" | custom-call | tf_op jit(solution)/shard_map/pallas_call | solution.py:381
  9.3 64.8 %shard_map.140 = (f32[4,512,256]{2,1,0:T(8,128)}, f32[8,256]{1,0:T(8,128)}) custom-call(bf16[3,256,512]{2,1,0:T(8,128)(2,1)} %get-tuple-element.8.high, bf16[3,256,512]{2,1,0:T(8,128)(2,1)} %get-tuple-element.9.low, f32[8,256]{1,0:T(8,128)} %get-tuple-element.10.sums, bf16[2,512,512]{2,1,0:T(8,128)(2,1)} %constant.8.clone.first, ...), custom_call_target="tpu_custom_call" | custom-call | tf_op jit(solution)/shard_map/pallas_call | solution.py:389
  74.1 4.8 %shard_map.141 = (f32[3,2,8,32,256]{4,3,2,1,0:T(8,128)}, f32[3,2,8,32,256]{4,3,2,1,0:T(8,128)}, f32[2,8]{1,0:T(2,128)}) custom-call(s32[8]{0:T(128)} %flag.3, s32[8]{0:T(128)} %amount.3, f32[1]{0:T(128)S(6)} %copy.15.viscosity, f32[1]{0:T(128)S(6)} %copy.16.shear, f32[1]{0:T(128)S(6)} %copy.17.clock, f32[1]{0:T(128)S(6)} %copy.18.time_step, ...), custom_call_target="tpu_custom_call" | custom-call | tf_op jit(solution)/shard_map/pallas_call | solution.py:404

commit v4 on v3

--- a/solution.py
+++ b/solution.py
@@ -12,7 +12,7 @@
 KX = 8 * ROWS
 F32 = jnp.float32
 BF16 = jnp.bfloat16
-VLIM = 60 * 1024 * 1024
+MIB = 1024 * 1024
 
 
 def halves(table):
@@ -96,8 +96,9 @@
         along = (wave[0] * v[0] + wave[1] * v[1] + wave[2] * v[2]) * inverse
         for c in range(3):
             high, low = split(jnp.where(mask, v[c] - wave[c] * along, 0.0))
-            high_out[c, :, p * N:(p + 1) * N] = high
-            low_out[c, :, p * N:(p + 1) * N] = low
+            slot = (0, 2, 1)[c]
+            high_out[slot, :, p * N:(p + 1) * N] = high
+            low_out[slot, :, p * N:(p + 1) * N] = low
     def total(value):
         value = jnp.sum(value, axis=0, keepdims=True)
         return value[:, :128] + value[:, 128:]
@@ -123,14 +124,20 @@
         ref = recv_f.at[0, pl.ds(0, 8 * blocks)]
         pltpu.make_async_copy(ref, ref, sem).wait()
 
+    to_cols = [lax.rem(col + j, 8) for j in range(8)]
+    spots = [lax.rem(col + j, 6) for j in range(6)]
+    on_cols = [spot + 2 * (spot // 3) for spot in spots]
     barrier = pltpu.get_barrier_semaphore()
 
     def greet(i, carry):
-        to = lax.rem(me + i, 128)
-        pl.semaphore_signal(barrier, inc=1, device_id={"row": to // 8, "col": lax.rem(to, 8)}, device_id_type=MESH)
+        to_row = lax.rem(row + i, 16)
+        for j in range(8):
+            @pl.when((i > 0) | (j > 0))
+            def _():
+                pl.semaphore_signal(barrier, inc=1, device_id={"row": to_row, "col": to_cols[j]}, device_id_type=MESH)
         return carry
 
-    lax.fori_loop(1, 128, greet, 0)
+    lax.fori_loop(0, 16, greet, 0)
     pl.semaphore_wait(barrier, 127)
     for i in range(1, 8):
         push(sums, recv_s.at[col], 7, {"col": (col + i) % 8}).start()
@@ -147,12 +154,15 @@
                             result[start:start + 128, 128 * h:128 * h + 128])
 
             def send(i, carry):
-                to = lax.rem(me + i, 128)
-                push(send_b.at[f, pl.ds(to * 8, 8)], recv_b.at[f, col, pl.ds(row * 8, 8)], f,
-                     {"row": to // 8, "col": lax.rem(to, 8)}).start()
+                to_row = lax.rem(row + i, 16)
+                for j in range(8):
+                    @pl.when((i > 0) | (j > 0))
+                    def _():
+                        push(send_b.at[f, pl.ds(to_row * 64 + to_cols[j] * 8, 8)],
+                             recv_b.at[f, col, pl.ds(row * 8, 8)], f, {"row": to_row, "col": to_cols[j]}).start()
                 return carry
 
-            lax.fori_loop(1, 128, send, 0)
+            lax.fori_loop(0, 16, send, 0)
             recv_b[f, col, pl.ds(row * 8, 8), :] = send_b[f, pl.ds(me * 8, 8), :]
             return carry
 
@@ -181,7 +191,7 @@
             u[f, :, plane * N:plane * N + N] = dot3((back[0], back[1]), split(both))
 
     def to_modes(t):
-        a = jnp.where((t == 0) | (t == 3), 0, jnp.where(t == 4, 2, 1))
+        a = jnp.where((t == 0) | (t == 2), 0, jnp.where(t == 4, 2, 1))
         b = jnp.where(t < 2, 1, 2)
         weight = jnp.where((t == 1) | (t == 4), 1.0, 0.0)
         planes = []
@@ -213,18 +223,15 @@
                     send_f[g, 4 * half + i] = moved[i]
 
         def send(i, carry):
-            number = lax.rem(me + i, 6 * ROWS)
-            to_row, spot = number // 6, lax.rem(number, 6)
-            to_col = spot + 2 * (spot // 3)
-
-            @pl.when((to_row != row) | (to_col != col))
-            def _():
-                push(send_f.at[g, to_col, pl.ds(to_row * 8, 8)], recv_f.at[g, pl.ds(me * 8, 8)], 3 + g,
-                     {"row": to_row, "col": to_col}).start()
-
+            to_row = lax.rem(row + i, ROWS)
+            for to_col in on_cols:
+                @pl.when((to_row != row) | (to_col != col))
+                def _():
+                    push(send_f.at[g, to_col, pl.ds(to_row * 8, 8)], recv_f.at[g, pl.ds(me * 8, 8)], 3 + g,
+                         {"row": to_row, "col": to_col}).start()
             return carry
 
-        lax.fori_loop(0, 6 * ROWS, send, 0)
+        lax.fori_loop(0, ROWS, send, 0)
 
         @pl.when(on)
         def _():
@@ -241,15 +248,18 @@
         def _():
             to_modes(jnp.where(step < 4, step - 2, step - 3))
 
-        @pl.when(step == 5)
-        def _():
-            field_out(0, lambda t: jnp.where(origin, t(0), kx * t(0) + kz * t(2)))
-            field_out(1, lambda t: jnp.where(origin, t(2), kz * t(0) - kx * t(2)))
+        @pl.when(step == 3)
+        def _():
+            field_out(0, lambda t: (kz * kz - kx * kx) * t(0) - kx * kz * t(1))
+
+        @pl.when(step == 6)
+        def _():
+            field_out(1, lambda t: jnp.where(origin, t(2), kx * t(2) + kz * t(3)))
+            field_out(2, lambda t: jnp.where(origin, t(3), kz * t(2) - kx * t(3)))
 
         @pl.when(step == 7)
         def _():
-            field_out(2, lambda t: (kz * kz - kx * kx) * t(3) - kx * kz * t(4))
-            field_out(3, lambda t: 2.0 * kx * kz * t(3) + kz * kz * t(4) - (kx * kx + kz * kz) * t(1))
+            field_out(3, lambda t: 2.0 * kx * kz * t(0) + kz * kz * t(1) - (kx * kx + kz * kz) * t(4))
 
         return carry
 
@@ -308,7 +318,7 @@
             value = jnp.sum(total[:, 128 * i:128 * i + 128], axis=1, keepdims=True) * (factor / (N * N))
             spectra[i:i + 1, :] = jnp.sum(jnp.where(diagonal, value, 0.0), axis=0, keepdims=True)
 
-    hats = [(block[g, :N], block[g, N:]) for g in (0, 3, 2, 1)]
+    hats = [(block[g, :N], block[g, N:]) for g in (1, 3, 0, 2)]
     lane = lax.broadcasted_iota(jnp.int32, (N, 128), 1)
     kx_index = lane // 32 + (row * 8 + step * 4)
     kz_index = lane % 32 + col * 32
@@ -351,7 +361,7 @@
                 new_velocity[c, p, i] = v[c] + (15.0 / 16.0) * fresh
 
 
-def call(kernel, grid, ins, outs, scratch=()):
+def call(kernel, grid, limit, ins, outs, scratch=()):
     return pl.pallas_call(
         kernel,
         grid=grid,
@@ -359,7 +369,7 @@
         out_specs=[spec for spec, _ in outs],
         out_shape=[shape for _, shape in outs],
         scratch_shapes=list(scratch),
-        compiler_params=pltpu.CompilerParams(vmem_limit_bytes=VLIM),
+        compiler_params=pltpu.CompilerParams(vmem_limit_bytes=limit * MIB),
     )
 
 
@@ -379,7 +389,7 @@
     first, second, back, fore = [jnp.asarray(table) for table in tables()]
     shape = jax.ShapeDtypeStruct
     high, low, sums = call(
-        pre_kernel, (8,),
+        pre_kernel, (8,), 8,
         [SMEM] * 4 + [spec((3, 2, 1, 32, N), lambda i: (0, 0, i, 0, 0))],
         [(spec((3, 32, 2 * N), lambda i: (0, i, 0)), shape((3, N, 2 * N), BF16)),
          (spec((3, 32, 2 * N), lambda i: (0, i, 0)), shape((3, N, 2 * N), BF16)),
@@ -398,11 +408,11 @@
             pltpu.VMEM((3, N, 2 * N), F32), pltpu.VMEM((5, 2 * KX, 2 * N), F32), pltpu.VMEM((2, 4 * KX, 128), F32),
             pltpu.SemaphoreType.DMA((8,)), pltpu.SemaphoreType.DMA((8,)),
         ],
-        compiler_params=pltpu.CompilerParams(collective_id=0, has_side_effects=True, vmem_limit_bytes=VLIM),
+        compiler_params=pltpu.CompilerParams(collective_id=0, has_side_effects=True, vmem_limit_bytes=32 * MIB),
     )(high, low, sums, first, second, back, fore)
     state = spec((3, 2, 4, 32, N), lambda i: (0, 0, i, 0, 0))
     return call(
-        post_kernel, (2,),
+        post_kernel, (2,), 20,
         [SMEM] * 6 + [spec((8, N), lambda i: (0, 0)), spec((4, 2 * N, 128), lambda i: (0, 0, i)), state, state],
         [(state, shape(velocity.shape, F32)), (state, shape(velocity.shape, F32)),
          (spec((2, 8), lambda i: (0, 0)), shape((2, 8), F32))],

time: 79.2 us -> 70.3 us (0.89)
  Pallas kernels: 75.7 us -> 62.8 us
  local copies, waits for them, and re-layouts: 0 us -> 3.96 us
    pallas_call x1, Pallas kernels: 64.8 us -> 56.6 us  [body(): pl.pallas_call(middle_kernel, in_specs=[vmem] * 7, out_specs=[vmem] * 2,...]
    pallas_call x2, Pallas kernels: 10.9 us -> 6.2 us  [the longest x1 3.84 us: body(): call(post_kernel, (2,), 20, [SMEM] * 6 + [spec((8, N), lambda i: (0, 0)),...]
    unnamed x0 -> x22, local copies, waits for them, and re-layouts: none -> 3.96 us
where the time goes in v4:
time: 70.3 us; the launch traced here: 70.1 us
  Pallas kernels  62.8 us (89%)
  local copies, waits for them, and re-layouts  3.96 us (6%)
  between operations  3.31 us (5%)
    pallas_call x1, Pallas kernels, body(): pl.pallas_call(middle_kernel, in_specs=[vmem] * 7, out_specs=[vmem] * 2,...  56.6 us
    unnamed x22, local copies, waits for them, and re-layouts  3.96 us
    pallas_call x1, Pallas kernels, body(): call(post_kernel, (2,), 20, [SMEM] * 6 + [spec((8, N), lambda i: (0, 0)),...  3.84 us
    pallas_call x1, Pallas kernels, body(): call(pre_kernel, (8,), 8, [SMEM] * 4 + [spec((3, 2, 1, 32, N), lambda i:...  2.36 us

profile of v4, /device:TPU:1, one launch (start us, length us, event | category | flops | bytes accessed | tf_op | source)
XLA Modules:
  0.0 70.1 jit_solution(11595719096162992160)
XLA Ops:
  3.2 0.0 copy-start
  3.2 1.4 %copy-done = f32[3,2,8,32,256]{4,3,2,1,0:T(8,128)S(1)} copy-done((f32[3,2,8,32,256]{4,3,2,1,0:T(8,128)S(1)}, f32[3,2,8,32,256]{4,3,2,1,0:T(8,128)}, u32[]{:S(2)}) %copy-start) | copy-done | bytes 1572888
  4.6 0.0 copy-start.7
  4.6 0.7 copy-done.7
  5.3 0.0 copy-start.9
  5.3 0.7 copy-done.9
  5.9 0.0 copy-start.3
  5.9 0.0 copy-start.5
  5.9 0.0 copy-start.6
  5.9 2.4 %shard_map.139 = (bf16[3,256,512]{2,1,0:T(8,128)(2,1)S(1)}, bf16[3,256,512]{2,1,0:T(8,128)(2,1)S(1)}, f32[8,256]{1,0:T(8,128)S(1)}) custom-call(s32[8]{0:T(128)S(1)} %copy-done.7, s32[8]{0:T(128)S(1)} %copy-done.9, f32[1]{0:T(128)S(6)} %copy.16.shear, f32[1]{0:T(128)S(6)} %copy.17.clock, f32[3,2,8,32,256]{4,3,2,1,0:T(8,128)S(1)} %copy-done), custom_call_target="tpu_custom_call" | custom-call | tf_op jit(solution)/shard_map/pallas_call | solution.py:391
  8.3 0.0 copy-done.3
  8.3 0.0 copy-done.5
  8.3 0.0 copy-done.6
  8.3 0.0 copy-start.4
  8.4 1.2 %copy-done.4 = bf16[2,512,512]{2,1,0:T(8,128)(2,1)S(1)} copy-done((bf16[2,512,512]{2,1,0:T(8,128)(2,1)S(1)}, bf16[2,512,512]{2,1,0:T(8,128)(2,1)}, u32[]{:S(2)}) %copy-start.4) | copy-done | bytes 1048600
  9.6 0.0 copy-start.1
  9.6 0.0 copy-start.2
  9.6 0.0 copy-start.8
  9.6 0.0 copy-start.10
  9.6 56.6 %shard_map.140 = (f32[4,512,256]{2,1,0:T(8,128)S(1)}, f32[8,256]{1,0:T(8,128)S(1)}) custom-call(bf16[3,256,512]{2,1,0:T(8,128)(2,1)S(1)} %get-tuple-element.8.high, bf16[3,256,512]{2,1,0:T(8,128)(2,1)S(1)} %get-tuple-element.9.low, f32[8,256]{1,0:T(8,128)S(1)} %get-tuple-element.10.sums, bf16[2,512,512]{2,1,0:T(8,128)(2,1)S(1)} %copy-done.4, ...), custom_call_target="tpu_custom_call" | custom-call | tf_op jit(solution)/shard_map/pallas_call | solution.py:399
  66.2 0.0 copy-done.1
  66.2 0.0 copy-done.2
  66.2 0.0 copy-done.8
  66.2 0.0 copy-done.10
  66.2 3.8 %shard_map.141 = (f32[3,2,8,32,256]{4,3,2,1,0:T(8,128)}, f32[3,2,8,32,256]{4,3,2,1,0:T(8,128)}, f32[2,8]{1,0:T(2,128)}) custom-call(s32[8]{0:T(128)S(1)} %copy-done.8, s32[8]{0:T(128)S(1)} %copy-done.10, f32[1]{0:T(128)S(6)} %copy.15.viscosity, f32[1]{0:T(128)S(6)} %copy.16.shear, f32[1]{0:T(128)S(6)} %copy.17.clock, f32[1]{0:T(128)S(6)} %copy.18.time_step, ...), custom_call_target="tpu_custom_call" | custom-call | tf_op jit(solution)/shard_map/pallas_call | solution.py:414
Async XLA Ops:
  3.2 1.4 %copy-start = (f32[3,2,8,32,256]{4,3,2,1,0:T(8,128)S(1)}, f32[3,2,8,32,256]{4,3,2,1,0:T(8,128)}, u32[]{:S(2)}) copy-start(f32[3,2,8,32,256]{4,3,2,1,0:T(8,128)} %velocity.3) | copy-start | bytes 4718596
  4.6 0.7 copy-start.7
  5.3 0.7 copy-start.9
  5.9 2.4 %copy-start.3 = (bf16[2,512,512]{2,1,0:T(8,128)(2,1)S(1)}, bf16[2,512,512]{2,1,0:T(8,128)(2,1)}, u32[]{:S(2)}) copy-start(bf16[2,512,512]{2,1,0:T(8,128)(2,1)} %constant.9.clone.second) | copy-start | bytes 3145732
  5.9 2.4 %copy-start.5 = (bf16[2,256,176]{2,1,0:T(8,128)(2,1)S(1)}, bf16[2,256,176]{2,1,0:T(8,128)(2,1)}, u32[]{:S(2)}) copy-start(bf16[2,256,176]{2,1,0:T(8,128)(2,1)} %constant.10.clone.back) | copy-start | bytes 540676
  5.9 2.4 %copy-start.6 = (bf16[2,176,256]{2,1,0:T(8,128)(2,1)S(1)}, bf16[2,176,256]{2,1,0:T(8,128)(2,1)}, u32[]{:S(2)}) copy-start(bf16[2,176,256]{2,1,0:T(8,128)(2,1)} %constant.11.clone.fore) | copy-start | bytes 540676
  8.3 1.2 %copy-start.4 = (bf16[2,512,512]{2,1,0:T(8,128)(2,1)S(1)}, bf16[2,512,512]{2,1,0:T(8,128)(2,1)}, u32[]{:S(2)}) copy-start(bf16[2,512,512]{2,1,0:T(8,128)(2,1)} %constant.8.clone.first) | copy-start | bytes 3145732
  9.6 56.6 %copy-start.1 = (f32[3,2,8,32,256]{4,3,2,1,0:T(8,128)S(1)}, f32[3,2,8,32,256]{4,3,2,1,0:T(8,128)}, u32[]{:S(2)}) copy-start(f32[3,2,8,32,256]{4,3,2,1,0:T(8,128)} %velocity.3) | copy-start | bytes 4718596
  9.6 56.7 %copy-start.2 = (f32[3,2,8,32,256]{4,3,2,1,0:T(8,128)S(1)}, f32[3,2,8,32,256]{4,3,2,1,0:T(8,128)}, u32[]{:S(2)}) copy-start(f32[3,2,8,32,256]{4,3,2,1,0:T(8,128)} %accumulator.1) | copy-start | bytes 4718596
  9.6 56.7 %copy-start.8 = (s32[8]{0:T(128)S(1)}, s32[8]{0:T(128)}, u32[]{:S(2)}) copy-start(s32[8]{0:T(128)} %flag.3) | copy-start | bytes 100
  9.6 56.7 %copy-start.10 = (s32[8]{0:T(128)S(1)}, s32[8]{0:T(128)}, u32[]{:S(2)}) copy-start(s32[8]{0:T(128)} %amount.3) | copy-start | bytes 100

commit v5 on v4

--- a/solution.py
+++ b/solution.py
@@ -78,38 +78,40 @@
     return wave_x, wave_y, wave_z, square, mask
 
 
-def pre_kernel(flag, amount, shear, clock, velocity, high_out, low_out, sums_out):
-    step = pl.program_id(0)
-    shift = (0 - flag[step] * amount[step]) & (N - 1)
-    kx = jnp.full((32, N), lax.axis_index("row") * 8 + step, jnp.int32)
-    kz = lax.broadcasted_iota(jnp.int32, (32, N), 0) + lax.axis_index("col") * 32
+def start_modes(kx_local, row, col, flag, amount, shear, clock, velocity, high, low, sums):
+    shift = (0 - flag[kx_local] * amount[kx_local]) & (N - 1)
+    kx = jnp.full((32, N), row * 8 + kx_local, jnp.int32)
+    kz = lax.broadcasted_iota(jnp.int32, (32, N), 0) + col * 32
     ky = lax.broadcasted_iota(jnp.int32, (32, N), 1)
     wave_x, wave_y, wave_z, square, mask = modes(kx, kz, ky, shear[0] * clock[0])
     inverse = 1.0 / jnp.maximum(square, 1.0)
     wave = (wave_x, wave_y, wave_z)
     energy = jnp.zeros((32, N), F32)
     stress = jnp.zeros((32, N), F32)
+    rows = pl.ds(pl.multiple_of(kx_local * 32, 32), 32)
     for p in range(2):
-        v = [pltpu.roll(velocity[c, p, 0], shift, 1) for c in range(3)]
+        v = [pltpu.roll(velocity[c, p, kx_local], shift, 1) for c in range(3)]
         energy += v[0] * v[0] + v[1] * v[1] + v[2] * v[2]
         stress += v[0] * v[1]
         along = (wave[0] * v[0] + wave[1] * v[1] + wave[2] * v[2]) * inverse
-        for c in range(3):
-            high, low = split(jnp.where(mask, v[c] - wave[c] * along, 0.0))
-            slot = (0, 2, 1)[c]
-            high_out[slot, :, p * N:(p + 1) * N] = high
-            low_out[slot, :, p * N:(p + 1) * N] = low
+        for slot, c in enumerate((0, 2, 1)):
+            upper, lower = split(jnp.where(mask, v[c] - wave[c] * along, 0.0))
+            high[slot, rows, p * N:(p + 1) * N] = upper
+            low[slot, rows, p * N:(p + 1) * N] = lower
+
     def total(value):
         value = jnp.sum(value, axis=0, keepdims=True)
         return value[:, :128] + value[:, 128:]
-    sums_out[pl.ds(step, 1), :] = jnp.concatenate([total(stress), total(square * energy)], axis=1)
+
+    sums[pl.ds(kx_local, 1), :] = jnp.concatenate([total(stress), total(square * energy)], axis=1)
 
 
 MESH = pl.DeviceIdType.MESH
 
 
-def middle_kernel(high, low, sums, first, second, back, fore, hats_out, total_out,
-                  send_b, recv_b, send_f, recv_f, recv_s, u, hats, data, out_sems, in_sems):
+def middle_kernel(flag_in, amount_in, shear, clock, velocity_in, first_in, second_in, back_in, fore_in,
+                  hats_out, total_out, flag, amount, velocity, first, second, back, fore, high, low, sums,
+                  send_b, recv_b, send_f, recv_f, recv_s, u, hats, data, out_sems, in_sems, load_sems):
     row, col = lax.axis_index("row"), lax.axis_index("col")
     me = row * 8 + col
     on = (row < ROWS) & (col != 3) & (col != 4)
@@ -137,7 +139,25 @@
                 pl.semaphore_signal(barrier, inc=1, device_id={"row": to_row, "col": to_cols[j]}, device_id_type=MESH)
         return carry
 
+    loads = [pltpu.make_async_copy(velocity_in.at[:, :, kx], velocity.at[:, :, kx], load_sems.at[kx]) for kx in range(8)]
+    for i, (source, target) in enumerate(((first_in, first), (second_in, second), (back_in, back), (fore_in, fore))):
+        loads.append(pltpu.make_async_copy(source, target, load_sems.at[8 + i]))
+    for i, (source, target) in enumerate(((flag_in, flag), (amount_in, amount))):
+        loads.append(pltpu.make_async_copy(source, target, load_sems.at[12 + i]))
+    for load in loads[12:] + loads[:12]:
+        load.start()
     lax.fori_loop(0, 16, greet, 0)
+
+    def prepare(kx, carry):
+        pltpu.make_async_copy(velocity_in.at[:, :, kx], velocity.at[:, :, kx], load_sems.at[kx]).wait()
+        start_modes(kx, row, col, flag, amount, shear, clock, velocity, high, low, sums)
+        return carry
+
+    for load in loads[12:]:
+        load.wait()
+    lax.fori_loop(0, 8, prepare, 0)
+    for load in loads[8:12]:
+        load.wait()
     pl.semaphore_wait(barrier, 127)
     for i in range(1, 8):
         push(sums, recv_s.at[col], 7, {"col": (col + i) % 8}).start()
@@ -388,31 +408,29 @@
 def body(velocity, accumulator, remesh_flag, remesh_shift, viscosity, shear, clock, step):
     first, second, back, fore = [jnp.asarray(table) for table in tables()]
     shape = jax.ShapeDtypeStruct
-    high, low, sums = call(
-        pre_kernel, (8,), 8,
-        [SMEM] * 4 + [spec((3, 2, 1, 32, N), lambda i: (0, 0, i, 0, 0))],
-        [(spec((3, 32, 2 * N), lambda i: (0, i, 0)), shape((3, N, 2 * N), BF16)),
-         (spec((3, 32, 2 * N), lambda i: (0, i, 0)), shape((3, N, 2 * N), BF16)),
-         (spec((8, N), lambda i: (0, 0)), shape((8, N), F32))],
-    )(remesh_flag, remesh_shift, shear, clock, velocity)
     vmem = pl.BlockSpec(memory_space=pltpu.VMEM)
+    hbm = pl.BlockSpec(memory_space=pltpu.HBM)
     hats, total = pl.pallas_call(
         middle_kernel,
-        in_specs=[vmem] * 7,
+        in_specs=[hbm] * 2 + [SMEM] * 2 + [hbm] * 5,
         out_specs=[vmem] * 2,
         out_shape=[shape((4, 2 * N, N), F32), shape((8, N), F32)],
         scratch_shapes=[
+            pltpu.SMEM((8,), jnp.int32), pltpu.SMEM((8,), jnp.int32),
+            pltpu.VMEM(velocity.shape, F32), pltpu.VMEM(first.shape, BF16), pltpu.VMEM(second.shape, BF16),
+            pltpu.VMEM(back.shape, BF16), pltpu.VMEM(fore.shape, BF16),
+            pltpu.VMEM((3, N, 2 * N), BF16), pltpu.VMEM((3, N, 2 * N), BF16), pltpu.VMEM((8, N), F32),
             pltpu.VMEM((3, 1024, 128), F32), pltpu.VMEM((3, 8, KX, 128), F32),
             pltpu.VMEM((4, 8, KX, 128), F32), pltpu.VMEM((4, 1024, 128), F32),
             pltpu.VMEM((8, 8, N), F32),
             pltpu.VMEM((3, N, 2 * N), F32), pltpu.VMEM((5, 2 * KX, 2 * N), F32), pltpu.VMEM((2, 4 * KX, 128), F32),
-            pltpu.SemaphoreType.DMA((8,)), pltpu.SemaphoreType.DMA((8,)),
+            pltpu.SemaphoreType.DMA((8,)), pltpu.SemaphoreType.DMA((8,)), pltpu.SemaphoreType.DMA((14,)),
         ],
-        compiler_params=pltpu.CompilerParams(collective_id=0, has_side_effects=True, vmem_limit_bytes=32 * MIB),
-    )(high, low, sums, first, second, back, fore)
+        compiler_params=pltpu.CompilerParams(collective_id=0, has_side_effects=True, vmem_limit_bytes=60 * MIB),
+    )(remesh_flag, remesh_shift, shear, clock, velocity, first, second, back, fore)
     state = spec((3, 2, 4, 32, N), lambda i: (0, 0, i, 0, 0))
     return call(
-        post_kernel, (2,), 20,
+        post_kernel, (2,), 60,
         [SMEM] * 6 + [spec((8, N), lambda i: (0, 0)), spec((4, 2 * N, 128), lambda i: (0, 0, i)), state, state],
         [(state, shape(velocity.shape, F32)), (state, shape(velocity.shape, F32)),
          (spec((2, 8), lambda i: (0, 0)), shape((2, 8), F32))],

time: 70.3 us -> 66.4 us (0.945)
  local copies, waits for them, and re-layouts: 3.96 us -> 0 us
    unnamed x22 -> x0, local copies, waits for them, and re-layouts: 3.96 us -> none
    pallas_call x3 -> x2, Pallas kernels: 62.8 us -> 63.1 us  [the longest x1 58.3 us: body(): pl.pallas_call(middle_kernel, in_specs=[hbm] * 2 + [SMEM] * 2 + [hbm] * 5...]
where the time goes in v5:
time: 66.4 us; the launch traced here: 66.3 us
  Pallas kernels  63.1 us (95%)
  between operations  3.22 us (5%)
    pallas_call x1, Pallas kernels, body(): pl.pallas_call(middle_kernel, in_specs=[hbm] * 2 + [SMEM] * 2 + [hbm] * 5...  58.3 us
    pallas_call x1, Pallas kernels, body(): call(post_kernel, (2,), 60, [SMEM] * 6 + [spec((8, N), lambda i: (0, 0)),...  4.8 us

profile of v5, /device:TPU:1, one launch (start us, length us, event | category | flops | bytes accessed | tf_op | source)
XLA Modules:
  0.0 66.3 jit_solution(3425062339271495580)
XLA Ops:
  3.2 58.3 %shard_map.139 = (f32[4,512,256]{2,1,0:T(8,128)}, f32[8,256]{1,0:T(8,128)}) custom-call(s32[8]{0:T(128)} %flag.1, s32[8]{0:T(128)} %amount.1, f32[1]{0:T(128)S(6)} %copy.16.shear, f32[1]{0:T(128)S(6)} %copy.17.clock, f32[3,2,8,32,256]{4,3,2,1,0:T(8,128)} %velocity.1, bf16[2,512,512]{2,1,0:T(8,128)(2,1)} %constant.8.clone.first_in, ...), custom_call_target="tpu_custom_call" | custom-call | tf_op jit(solution)/shard_map/pallas_call | solution.py:413
  61.5 4.8 %shard_map.140 = (f32[3,2,8,32,256]{4,3,2,1,0:T(8,128)}, f32[3,2,8,32,256]{4,3,2,1,0:T(8,128)}, f32[2,8]{1,0:T(2,128)}) custom-call(s32[8]{0:T(128)} %flag.1, s32[8]{0:T(128)} %amount.1, f32[1]{0:T(128)S(6)} %copy.15.viscosity, f32[1]{0:T(128)S(6)} %copy.16.shear, f32[1]{0:T(128)S(6)} %copy.17.clock, f32[1]{0:T(128)S(6)} %copy.18.time_step, ...), custom_call_target="tpu_custom_call" | custom-call | tf_op jit(solution)/shard_map/pallas_call | solution.py:432

commit v6 on v5

--- a/solution.py
+++ b/solution.py
@@ -10,6 +10,7 @@
 ROWS = 11
 COLS = (0, 1, 2, 5, 6, 7)
 KX = 8 * ROWS
+BACK = 2 * 192
 F32 = jnp.float32
 BF16 = jnp.bfloat16
 MIB = 1024 * 1024
@@ -78,39 +79,47 @@
     return wave_x, wave_y, wave_z, square, mask
 
 
-def start_modes(kx_local, row, col, flag, amount, shear, clock, velocity, high, low, sums):
+def remeshed_modes(kx_local, row, col, flag, amount, shear, clock, velocity):
     shift = (0 - flag[kx_local] * amount[kx_local]) & (N - 1)
     kx = jnp.full((32, N), row * 8 + kx_local, jnp.int32)
     kz = lax.broadcasted_iota(jnp.int32, (32, N), 0) + col * 32
     ky = lax.broadcasted_iota(jnp.int32, (32, N), 1)
-    wave_x, wave_y, wave_z, square, mask = modes(kx, kz, ky, shear[0] * clock[0])
+    state = [[pltpu.roll(velocity[c, p, kx_local], shift, 1) for c in range(3)] for p in range(2)]
+    return state, modes(kx, kz, ky, shear[0] * clock[0])
+
+
+def project_modes(kx_local, state, waves, high, low):
+    wave, square, mask = waves[:3], waves[3], waves[4]
     inverse = 1.0 / jnp.maximum(square, 1.0)
-    wave = (wave_x, wave_y, wave_z)
-    energy = jnp.zeros((32, N), F32)
-    stress = jnp.zeros((32, N), F32)
     rows = pl.ds(pl.multiple_of(kx_local * 32, 32), 32)
     for p in range(2):
-        v = [pltpu.roll(velocity[c, p, kx_local], shift, 1) for c in range(3)]
-        energy += v[0] * v[0] + v[1] * v[1] + v[2] * v[2]
-        stress += v[0] * v[1]
+        v = state[p]
         along = (wave[0] * v[0] + wave[1] * v[1] + wave[2] * v[2]) * inverse
         for slot, c in enumerate((0, 2, 1)):
             upper, lower = split(jnp.where(mask, v[c] - wave[c] * along, 0.0))
             high[slot, rows, p * N:(p + 1) * N] = upper
             low[slot, rows, p * N:(p + 1) * N] = lower
 
+
+def add_spectra(kx_local, state, waves, sums):
+    energy = jnp.zeros((32, N), F32)
+    stress = jnp.zeros((32, N), F32)
+    for v in state:
+        energy += v[0] * v[0] + v[1] * v[1] + v[2] * v[2]
+        stress += v[0] * v[1]
+
     def total(value):
         value = jnp.sum(value, axis=0, keepdims=True)
         return value[:, :128] + value[:, 128:]
 
-    sums[pl.ds(kx_local, 1), :] = jnp.concatenate([total(stress), total(square * energy)], axis=1)
+    sums[pl.ds(kx_local, 1), :] = jnp.concatenate([total(stress), total(waves[3] * energy)], axis=1)
 
 
 MESH = pl.DeviceIdType.MESH
 
 
 def middle_kernel(flag_in, amount_in, shear, clock, velocity_in, first_in, second_in, back_in, fore_in,
-                  hats_out, total_out, flag, amount, velocity, first, second, back, fore, high, low, sums,
+                  hats_out, flag, amount, result, velocity, first, second, back, fore, high, low, sums,
                   send_b, recv_b, send_f, recv_f, recv_s, u, hats, data, out_sems, in_sems, load_sems):
     row, col = lax.axis_index("row"), lax.axis_index("col")
     me = row * 8 + col
@@ -150,7 +159,11 @@
 
     def prepare(kx, carry):
         pltpu.make_async_copy(velocity_in.at[:, :, kx], velocity.at[:, :, kx], load_sems.at[kx]).wait()
-        start_modes(kx, row, col, flag, amount, shear, clock, velocity, high, low, sums)
+
+        @pl.when(on)
+        def _():
+            project_modes(kx, *remeshed_modes(kx, row, col, flag, amount, shear, clock, velocity), high, low)
+
         return carry
 
     for load in loads[12:]:
@@ -159,9 +172,6 @@
     for load in loads[8:12]:
         load.wait()
     pl.semaphore_wait(barrier, 127)
-    for i in range(1, 8):
-        push(sums, recv_s.at[col], 7, {"col": (col + i) % 8}).start()
-
     @pl.when(on)
     def _():
         def y_back(f, carry):
@@ -187,6 +197,14 @@
             return carry
 
         lax.fori_loop(0, 3, y_back, 0)
+
+    def spectra_of(kx, carry):
+        add_spectra(kx, *remeshed_modes(kx, row, col, flag, amount, shear, clock, velocity), sums)
+        return carry
+
+    lax.fori_loop(0, 8, spectra_of, 0)
+    for i in range(1, 8):
+        push(sums, recv_s.at[col], 7, {"col": (col + i) % 8}).start()
 
     def to_grid(f):
         @pl.when(on)
@@ -291,7 +309,8 @@
     total = recv_s[0]
     for i in range(1, 8):
         total = total + recv_s[i]
-    total_out[...] = total
+    for g in range(4):
+        result[g, BACK:BACK + 8, :] = total
 
     @pl.when(on)
     def _():
@@ -300,7 +319,9 @@
             both = jnp.concatenate(
                 [jnp.concatenate([recv_f[g, pl.ds((h * 2 + plane) * 2 + p, 128, stride=8), :] for h in range(2)], axis=1)
                  for p in range(2) for plane in range(2)], axis=0)
-            hats_out[g] = dot3((second[0], second[1]), split(both))
+            table = [jnp.concatenate([second[i, start:start + 96] for start in (0, 160, 256, 416)], axis=0) for i in range(2)]
+            result[g, :BACK, :] = dot3(table, split(both))
+            pltpu.make_async_copy(result.at[g], hats_out.at[g], load_sems.at[g]).start()
             return carry
 
         lax.fori_loop(0, 4, y_fore, 0)
@@ -308,7 +329,11 @@
     @pl.when(off)
     def _():
         for g in range(4):
-            hats_out[g] = jnp.zeros((2 * N, N), F32)
+            result[g, :BACK, :] = jnp.zeros((BACK, N), F32)
+            pltpu.make_async_copy(result.at[g], hats_out.at[g], load_sems.at[g]).start()
+
+    for g in range(4):
+        pltpu.make_async_copy(result.at[g], hats_out.at[g], load_sems.at[g]).wait()
 
     pltpu.make_async_copy(drain_sums, drain_sums, out_sems.at[7]).wait()
 
@@ -325,24 +350,23 @@
             drain(66, out_sems.at[3 + g])
 
 
-def post_kernel(flag, amount, viscosity, shear, clock, time_step, total, block, velocity, accumulator,
+def post_kernel(flag, amount, viscosity, shear, clock, time_step, block, velocity, accumulator,
                 new_velocity, new_accumulator, spectra):
     step = pl.program_id(0)
     row, col = lax.axis_index("row"), lax.axis_index("col")
     drift = shear[0] * clock[0]
 
-    @pl.when(step == 0)
-    def _():
-        diagonal = lax.broadcasted_iota(jnp.int32, (8, 8), 0) == lax.broadcasted_iota(jnp.int32, (8, 8), 1)
-        for i, factor in enumerate((1.0, 2.0 * viscosity[0])):
-            value = jnp.sum(total[:, 128 * i:128 * i + 128], axis=1, keepdims=True) * (factor / (N * N))
-            spectra[i:i + 1, :] = jnp.sum(jnp.where(diagonal, value, 0.0), axis=0, keepdims=True)
-
-    hats = [(block[g, :N], block[g, N:]) for g in (1, 3, 0, 2)]
-    lane = lax.broadcasted_iota(jnp.int32, (N, 128), 1)
+    diagonal = lax.broadcasted_iota(jnp.int32, (8, 8), 0) == lax.broadcasted_iota(jnp.int32, (8, 8), 1)
+    factor = jnp.where(step == 0, 1.0, 2.0 * viscosity[0]) / (N * N)
+    value = jnp.sum(block[0, BACK:BACK + 8, :], axis=1, keepdims=True) * factor
+    spectra[pl.ds(step, 1), :] = jnp.sum(jnp.where(diagonal, value, 0.0), axis=0, keepdims=True)
+
+    hats = [(block[g, :192], block[g, 192:384]) for g in (1, 3, 0, 2)]
+    lane = lax.broadcasted_iota(jnp.int32, (192, 128), 1)
     kx_index = lane // 32 + (row * 8 + step * 4)
     kz_index = lane % 32 + col * 32
-    ky_index = lax.broadcasted_iota(jnp.int32, (N, 128), 0)
+    place = lax.broadcasted_iota(jnp.int32, (192, 128), 0)
+    ky_index = jnp.where(place < 96, place, place + 64)
     kx, k1, kz, square, mask = modes(kx_index, kz_index, ky_index, drift)
     flat = kx * kx + kz * kz
     origin = flat == 0.0
@@ -360,7 +384,8 @@
             jnp.where(origin, 0.0 - k1 * s, (0.0 - kx * w - kz * k1 * v) * over_flat),
         ]
         for c in range(3):
-            result[c][p] = jnp.where(mask, part[c], 0.0).T
+            kept = jnp.where(mask, part[c], 0.0)
+            result[c][p] = jnp.concatenate([kept[:96], jnp.zeros((64, 128), F32), kept[96:]], axis=0).T
     for i in range(4):
         shift = (0 - flag[step * 4 + i] * amount[step * 4 + i]) & (N - 1)
         kx_index = jnp.full((32, N), row * 8 + step * 4 + i, jnp.int32)
@@ -408,15 +433,14 @@
 def body(velocity, accumulator, remesh_flag, remesh_shift, viscosity, shear, clock, step):
     first, second, back, fore = [jnp.asarray(table) for table in tables()]
     shape = jax.ShapeDtypeStruct
-    vmem = pl.BlockSpec(memory_space=pltpu.VMEM)
     hbm = pl.BlockSpec(memory_space=pltpu.HBM)
-    hats, total = pl.pallas_call(
+    [hats] = pl.pallas_call(
         middle_kernel,
         in_specs=[hbm] * 2 + [SMEM] * 2 + [hbm] * 5,
-        out_specs=[vmem] * 2,
-        out_shape=[shape((4, 2 * N, N), F32), shape((8, N), F32)],
+        out_specs=[hbm],
+        out_shape=[shape((4, BACK + 8, N), F32)],
         scratch_shapes=[
-            pltpu.SMEM((8,), jnp.int32), pltpu.SMEM((8,), jnp.int32),
+            pltpu.SMEM((8,), jnp.int32), pltpu.SMEM((8,), jnp.int32), pltpu.VMEM((4, BACK + 8, N), F32),
             pltpu.VMEM(velocity.shape, F32), pltpu.VMEM(first.shape, BF16), pltpu.VMEM(second.shape, BF16),
             pltpu.VMEM(back.shape, BF16), pltpu.VMEM(fore.shape, BF16),
             pltpu.VMEM((3, N, 2 * N), BF16), pltpu.VMEM((3, N, 2 * N), BF16), pltpu.VMEM((8, N), F32),
@@ -430,11 +454,11 @@
     )(remesh_flag, remesh_shift, shear, clock, velocity, first, second, back, fore)
     state = spec((3, 2, 4, 32, N), lambda i: (0, 0, i, 0, 0))
     return call(
-        post_kernel, (2,), 60,
-        [SMEM] * 6 + [spec((8, N), lambda i: (0, 0)), spec((4, 2 * N, 128), lambda i: (0, 0, i)), state, state],
+        post_kernel, (2,), 50,
+        [SMEM] * 6 + [spec((4, BACK + 8, 128), lambda i: (0, 0, i)), state, state],
         [(state, shape(velocity.shape, F32)), (state, shape(velocity.shape, F32)),
          (spec((2, 8), lambda i: (0, 0)), shape((2, 8), F32))],
-    )(remesh_flag, remesh_shift, viscosity, shear, clock, step, total, hats, velocity, accumulator)
+    )(remesh_flag, remesh_shift, viscosity, shear, clock, step, hats, velocity, accumulator)
 
 
 def solution(mesh):

time: 66.4 us -> 65.1 us (0.980)
  Pallas kernels: 63.1 us -> 61.6 us
    pallas_call x1, Pallas kernels: 4.8 us -> 4.04 us  [body(): call(post_kernel, (2,), 50, [SMEM] * 6 + [spec((4, BACK + 8, 128), lambda...]
    pallas_call x1, Pallas kernels: 58.3 us -> 57.6 us  [body(): pl.pallas_call(middle_kernel, in_specs=[hbm] * 2 + [SMEM] * 2 + [hbm] * 5...]
where the time goes in v6:
time: 65.1 us; the launch traced here: 64.9 us
  Pallas kernels  61.6 us (95%)
  between operations  3.29 us (5%)
    pallas_call x1, Pallas kernels, body(): pl.pallas_call(middle_kernel, in_specs=[hbm] * 2 + [SMEM] * 2 + [hbm] * 5...  57.6 us
    pallas_call x1, Pallas kernels, body(): call(post_kernel, (2,), 50, [SMEM] * 6 + [spec((4, BACK + 8, 128), lambda...  4.04 us

profile of v6, /device:TPU:1, one launch (start us, length us, event | category | flops | bytes accessed | tf_op | source)
XLA Modules:
  0.0 64.9 jit_solution(11802008877125816353)
XLA Ops:
  3.2 0.0 copy-start
  3.2 0.0 copy-start.1
  3.2 0.0 copy-start.2
  3.2 0.0 copy-start.3
  3.3 57.6 %shard_map.139.block = f32[4,392,256]{2,1,0:T(8,128)} custom-call(s32[8]{0:T(128)} %flag.1, s32[8]{0:T(128)} %amount.1, f32[1]{0:T(128)S(6)} %copy.16.shear, f32[1]{0:T(128)S(6)} %copy.17.clock, f32[3,2,8,32,256]{4,3,2,1,0:T(8,128)} %velocity.1, bf16[2,512,512]{2,1,0:T(8,128)(2,1)} %constant.8.clone.first_in, bf16[2,512,512]{2,1,0:T(8,128)(2,1)} %constant.9.clone.second_in, ...), custom_call_target="tpu_custom_call" | custom-call | tf_op jit(solution)/shard_map/pallas_call | solution.py:437
  60.9 0.0 copy-done
  60.9 0.0 copy-done.1
  60.9 0.0 copy-done.2
  60.9 0.0 copy-done.3
  60.9 4.0 %shard_map.140 = (f32[3,2,8,32,256]{4,3,2,1,0:T(8,128)}, f32[3,2,8,32,256]{4,3,2,1,0:T(8,128)}, f32[2,8]{1,0:T(2,128)}) custom-call(s32[8]{0:T(128)S(1)} %copy-done.2, s32[8]{0:T(128)S(1)} %copy-done.3, f32[1]{0:T(128)S(6)} %copy.15.viscosity, f32[1]{0:T(128)S(6)} %copy.16.shear, f32[1]{0:T(128)S(6)} %copy.17.clock, f32[1]{0:T(128)S(6)} %copy.18.time_step, ...), custom_call_target="tpu_custom_call" | custom-call | tf_op jit(solution)/shard_map/pallas_call | solution.py:456
Async XLA Ops:
  3.2 57.7 %copy-start = (f32[3,2,8,32,256]{4,3,2,1,0:T(8,128)S(1)}, f32[3,2,8,32,256]{4,3,2,1,0:T(8,128)}, u32[]{:S(2)}) copy-start(f32[3,2,8,32,256]{4,3,2,1,0:T(8,128)} %velocity.1) | copy-start | bytes 4718596
  3.2 57.7 %copy-start.1 = (f32[3,2,8,32,256]{4,3,2,1,0:T(8,128)S(1)}, f32[3,2,8,32,256]{4,3,2,1,0:T(8,128)}, u32[]{:S(2)}) copy-start(f32[3,2,8,32,256]{4,3,2,1,0:T(8,128)} %accumulator.1) | copy-start | bytes 4718596
  3.2 57.7 %copy-start.2 = (s32[8]{0:T(128)S(1)}, s32[8]{0:T(128)}, u32[]{:S(2)}) copy-start(s32[8]{0:T(128)} %flag.1) | copy-start | bytes 100
  3.2 57.7 %copy-start.3 = (s32[8]{0:T(128)S(1)}, s32[8]{0:T(128)}, u32[]{:S(2)}) copy-start(s32[8]{0:T(128)} %amount.1) | copy-start | bytes 100

commit v7 on v6

--- a/solution.py
+++ b/solution.py
@@ -119,7 +119,7 @@
 
 
 def middle_kernel(flag_in, amount_in, shear, clock, velocity_in, first_in, second_in, back_in, fore_in,
-                  hats_out, flag, amount, result, velocity, first, second, back, fore, high, low, sums,
+                  hats_out, flag, amount, result, kept, velocity, first, second, back, fore, high, low, sums,
                   send_b, recv_b, send_f, recv_f, recv_s, u, hats, data, out_sems, in_sems, load_sems):
     row, col = lax.axis_index("row"), lax.axis_index("col")
     me = row * 8 + col
@@ -203,6 +203,9 @@
         return carry
 
     lax.fori_loop(0, 8, spectra_of, 0)
+    for i in range(2):
+        for place, start in enumerate((0, 160, 256, 416)):
+            kept[i, 96 * place:96 * place + 96, :] = second[i, start:start + 96, :]
     for i in range(1, 8):
         push(sums, recv_s.at[col], 7, {"col": (col + i) % 8}).start()
 
@@ -319,8 +322,7 @@
             both = jnp.concatenate(
                 [jnp.concatenate([recv_f[g, pl.ds((h * 2 + plane) * 2 + p, 128, stride=8), :] for h in range(2)], axis=1)
                  for p in range(2) for plane in range(2)], axis=0)
-            table = [jnp.concatenate([second[i, start:start + 96] for start in (0, 160, 256, 416)], axis=0) for i in range(2)]
-            result[g, :BACK, :] = dot3(table, split(both))
+            result[g, :BACK, :] = dot3((kept[0], kept[1]), split(both))
             pltpu.make_async_copy(result.at[g], hats_out.at[g], load_sems.at[g]).start()
             return carry
 
@@ -440,7 +442,7 @@
         out_specs=[hbm],
         out_shape=[shape((4, BACK + 8, N), F32)],
         scratch_shapes=[
-            pltpu.SMEM((8,), jnp.int32), pltpu.SMEM((8,), jnp.int32), pltpu.VMEM((4, BACK + 8, N), F32),
+            pltpu.SMEM((8,), jnp.int32), pltpu.SMEM((8,), jnp.int32), pltpu.VMEM((4, BACK + 8, N), F32), pltpu.VMEM((2, BACK, 2 * N), BF16),
             pltpu.VMEM(velocity.shape, F32), pltpu.VMEM(first.shape, BF16), pltpu.VMEM(second.shape, BF16),
             pltpu.VMEM(back.shape, BF16), pltpu.VMEM(fore.shape, BF16),
             pltpu.VMEM((3, N, 2 * N), BF16), pltpu.VMEM((3, N, 2 * N), BF16), pltpu.VMEM((8, N), F32),

time: 65.1 us -> 65.1 us (level)
  no operation moved by 1% of the time
where the time goes in v7:
time: 65.1 us; the launch traced here: 64.9 us
  Pallas kernels  61.6 us (95%)
  between operations  3.29 us (5%)
    pallas_call x1, Pallas kernels, body(): pl.pallas_call(middle_kernel, in_specs=[hbm] * 2 + [SMEM] * 2 + [hbm] * 5...  57.6 us
    pallas_call x1, Pallas kernels, body(): call(post_kernel, (2,), 50, [SMEM] * 6 + [spec((4, BACK + 8, 128), lambda...  4.04 us

profile of v7, /device:TPU:1, one launch (start us, length us, event | category | flops | bytes accessed | tf_op | source)
XLA Modules:
  0.0 64.9 jit_solution(4052569550362846038)
XLA Ops:
  3.2 0.0 copy-start
  3.2 0.0 copy-start.1
  3.2 0.0 copy-start.2
  3.2 0.0 copy-start.3
  3.3 57.6 %shard_map.139.block = f32[4,392,256]{2,1,0:T(8,128)} custom-call(s32[8]{0:T(128)} %flag.1, s32[8]{0:T(128)} %amount.1, f32[1]{0:T(128)S(6)} %copy.16.shear, f32[1]{0:T(128)S(6)} %copy.17.clock, f32[3,2,8,32,256]{4,3,2,1,0:T(8,128)} %velocity.1, bf16[2,512,512]{2,1,0:T(8,128)(2,1)} %constant.8.clone.first_in, bf16[2,512,512]{2,1,0:T(8,128)(2,1)} %constant.9.clone.second_in, ...), custom_call_target="tpu_custom_call" | custom-call | tf_op jit(solution)/shard_map/pallas_call | solution.py:439
  60.9 0.0 copy-done
  60.9 0.0 copy-done.1
  60.9 0.0 copy-done.2
  60.9 0.0 copy-done.3
  60.9 4.0 %shard_map.140 = (f32[3,2,8,32,256]{4,3,2,1,0:T(8,128)}, f32[3,2,8,32,256]{4,3,2,1,0:T(8,128)}, f32[2,8]{1,0:T(2,128)}) custom-call(s32[8]{0:T(128)S(1)} %copy-done.2, s32[8]{0:T(128)S(1)} %copy-done.3, f32[1]{0:T(128)S(6)} %copy.15.viscosity, f32[1]{0:T(128)S(6)} %copy.16.shear, f32[1]{0:T(128)S(6)} %copy.17.clock, f32[1]{0:T(128)S(6)} %copy.18.time_step, ...), custom_call_target="tpu_custom_call" | custom-call | tf_op jit(solution)/shard_map/pallas_call | solution.py:458
Async XLA Ops:
  3.2 57.6 %copy-start = (f32[3,2,8,32,256]{4,3,2,1,0:T(8,128)S(1)}, f32[3,2,8,32,256]{4,3,2,1,0:T(8,128)}, u32[]{:S(2)}) copy-start(f32[3,2,8,32,256]{4,3,2,1,0:T(8,128)} %velocity.1) | copy-start | bytes 4718596
  3.2 57.6 %copy-start.1 = (f32[3,2,8,32,256]{4,3,2,1,0:T(8,128)S(1)}, f32[3,2,8,32,256]{4,3,2,1,0:T(8,128)}, u32[]{:S(2)}) copy-start(f32[3,2,8,32,256]{4,3,2,1,0:T(8,128)} %accumulator.1) | copy-start | bytes 4718596
  3.2 57.6 %copy-start.2 = (s32[8]{0:T(128)S(1)}, s32[8]{0:T(128)}, u32[]{:S(2)}) copy-start(s32[8]{0:T(128)} %flag.1) | copy-start | bytes 100
  3.2 57.6 %copy-start.3 = (s32[8]{0:T(128)S(1)}, s32[8]{0:T(128)}, u32[]{:S(2)}) copy-start(s32[8]{0:T(128)} %amount.1) | copy-start | bytes 100

commit v8 on v6

--- a/solution.py
+++ b/solution.py
@@ -168,7 +168,7 @@
 
     for load in loads[12:]:
         load.wait()
-    lax.fori_loop(0, 8, prepare, 0)
+    lax.fori_loop(0, 8, prepare, 0, unroll=2)
     for load in loads[8:12]:
         load.wait()
     pl.semaphore_wait(barrier, 127)

time: 65.1 us -> 65.1 us (level)
  no operation moved by 1% of the time
where the time goes in v8:
time: 65.1 us; the launch traced here: 64.9 us
  Pallas kernels  61.6 us (95%)
  between operations  3.29 us (5%)
    pallas_call x1, Pallas kernels, body(): pl.pallas_call(middle_kernel, in_specs=[hbm] * 2 + [SMEM] * 2 + [hbm] * 5...  57.6 us
    pallas_call x1, Pallas kernels, body(): call(post_kernel, (2,), 50, [SMEM] * 6 + [spec((4, BACK + 8, 128), lambda...  4.04 us

profile of v8, /device:TPU:1, one launch (start us, length us, event | category | flops | bytes accessed | tf_op | source)
XLA Modules:
  0.0 64.9 jit_solution(11357344446997816068)
XLA Ops:
  3.2 0.0 copy-start
  3.2 0.0 copy-start.1
  3.2 0.0 copy-start.2
  3.2 0.0 copy-start.3
  3.3 57.6 %shard_map.139.block = f32[4,392,256]{2,1,0:T(8,128)} custom-call(s32[8]{0:T(128)} %flag.1, s32[8]{0:T(128)} %amount.1, f32[1]{0:T(128)S(6)} %copy.16.shear, f32[1]{0:T(128)S(6)} %copy.17.clock, f32[3,2,8,32,256]{4,3,2,1,0:T(8,128)} %velocity.1, bf16[2,512,512]{2,1,0:T(8,128)(2,1)} %constant.8.clone.first_in, bf16[2,512,512]{2,1,0:T(8,128)(2,1)} %constant.9.clone.second_in, ...), custom_call_target="tpu_custom_call" | custom-call | tf_op jit(solution)/shard_map/pallas_call | solution.py:437
  60.9 0.0 copy-done
  60.9 0.0 copy-done.1
  60.9 0.0 copy-done.2
  60.9 0.0 copy-done.3
  60.9 4.0 %shard_map.140 = (f32[3,2,8,32,256]{4,3,2,1,0:T(8,128)}, f32[3,2,8,32,256]{4,3,2,1,0:T(8,128)}, f32[2,8]{1,0:T(2,128)}) custom-call(s32[8]{0:T(128)S(1)} %copy-done.2, s32[8]{0:T(128)S(1)} %copy-done.3, f32[1]{0:T(128)S(6)} %copy.15.viscosity, f32[1]{0:T(128)S(6)} %copy.16.shear, f32[1]{0:T(128)S(6)} %copy.17.clock, f32[1]{0:T(128)S(6)} %copy.18.time_step, ...), custom_call_target="tpu_custom_call" | custom-call | tf_op jit(solution)/shard_map/pallas_call | solution.py:456
Async XLA Ops:
  3.2 57.7 %copy-start = (f32[3,2,8,32,256]{4,3,2,1,0:T(8,128)S(1)}, f32[3,2,8,32,256]{4,3,2,1,0:T(8,128)}, u32[]{:S(2)}) copy-start(f32[3,2,8,32,256]{4,3,2,1,0:T(8,128)} %velocity.1) | copy-start | bytes 4718596
  3.2 57.7 %copy-start.1 = (f32[3,2,8,32,256]{4,3,2,1,0:T(8,128)S(1)}, f32[3,2,8,32,256]{4,3,2,1,0:T(8,128)}, u32[]{:S(2)}) copy-start(f32[3,2,8,32,256]{4,3,2,1,0:T(8,128)} %accumulator.1) | copy-start | bytes 4718596
  3.2 57.7 %copy-start.2 = (s32[8]{0:T(128)S(1)}, s32[8]{0:T(128)}, u32[]{:S(2)}) copy-start(s32[8]{0:T(128)} %flag.1) | copy-start | bytes 100
  3.2 57.7 %copy-start.3 = (s32[8]{0:T(128)S(1)}, s32[8]{0:T(128)}, u32[]{:S(2)}) copy-start(s32[8]{0:T(128)} %amount.1) | copy-start | bytes 100
